TPU v7x, 32 devices: a whole 2x2x4 slice. The times are simulated.
32 devices in a mesh: grp: 2 (over y), ep: 8 (over z, x), tp: 2 (over core).
Axes of the slice: x: 2, y: 2, z: 4, core: 2. Of those that a mesh axis runs over, the one named last changes fastest.
Arguments:
- queries: bfloat16 [1024, 16, 576], P(('grp', 'ep'), 'tp'), parts along dimension 0, may hold values from -450 to 450
- latent_cache: bfloat16 [48, 512, 576], P(('grp', 'ep'), 'tp'), parts along dimension 0, may hold values from -6 to 6
- residual: bfloat16 [1024, 2048], P(('grp', 'ep')), parts along dimension 0, may hold values from -8 to 8
- token_request: int32 [1024], P(('grp', 'ep')), parts along dimension 0, may hold values from 0 to 2, as said below
- token_visible: int32 [1024], P(('grp', 'ep')), parts along dimension 0, may hold values from 1 to 512, as said below
- value_proj: bfloat16 [16, 512, 128], P('tp', 'ep'), may hold values from -0.25 to 0.25
- out_proj: bfloat16 [2048, 2048], P('tp', 'ep'), may hold values from -0.125 to 0.125
- norm_gain: float32 [2048], replicated, may hold values from 0.1 to 1.9
- router: bfloat16 [2048, 64], replicated, may hold values from -0.0390625 to 0.0390625
- expert_ids: int32 [1024, 6], P(('grp', 'ep')), parts along dimension 0, may hold values from 0 to 63, all different within a row; in each aligned block of 64 rows (0 to 63, 64 to 127, ...) at most 8 rows name the same one
- gate_weight: bfloat16 [128, 2048, 384], P('ep', None, 'tp'), may hold values from -0.125 to 0.125
- up_weight: bfloat16 [128, 2048, 384], P('ep', None, 'tp'), may hold values from -0.125 to 0.125
- down_weight: bfloat16 [128, 384, 2048], P('ep', 'tp'), may hold values from -0.21875 to 0.21875
Outputs:
- hidden: bfloat16 [1024, 2048], P(('grp', 'ep'), 'tp'), parts along dimension 0
- expert_out: bfloat16 [1024, 2048], P(('grp', 'ep'), 'tp'), parts along dimension 0
There are 2 independent parts, one for each index of `grp`. A program takes and returns all parts, laid end to end along the dimension named above; an argument that names none is the same for every part. Nothing has to cross between parts.
Inputs may be any that keep to these rules, and one draw needn't show every extreme that they name: `token_request`: in each ep block, 62 tokens belong to request 0, a prefill span, and each other request has exactly one token; the tokens' order in the block is arbitrary. `token_visible`: the span's tokens read consecutive counts s + 1 to s + 62; 512 is reached in every draw. `expert_ids`: each row names 6 different experts; among the 64 tokens of one ep index no expert is named by more than 8 tokens, and this bound is reached.
All inputs are finite; a program needn't handle non-finite values.
Results may differ from a plain program's by a relative error of at most 0.018.
Values may be sent and summed in bfloat16 or wider, within the bound.
A program may use at most 128 MiB of HBM per device.

v0:
```python
import functools

import jax
import jax.numpy as jnp
from jax import lax
from jax.experimental import pallas as pl
from jax.experimental.pallas import tpu as pltpu
from jax.sharding import PartitionSpec as P

LATENT = 512
VDIM = 128
EXPERTS = 64
TOPK = 6
GROUPS = 2
CAP = 8
PIECES = 128
MESH = pl.DeviceIdType.MESH


score_scale = 192.0 ** (-0.5)
epsilon = 1e-06


def masked_scores(queries, block_rows, token_request, token_visible):
    per_request = block_rows.shape[1]
    flat_rows = block_rows.reshape(-1, block_rows.shape[2])
    scores = (
        jnp.einsum("thc,kc->thk", queries, flat_rows, preferred_element_type=jnp.float32)
        * score_scale
    )
    column = jnp.arange(flat_rows.shape[0], dtype=jnp.int32)
    owner_id = column // per_request
    position = column % per_request
    allowed = (owner_id[None, :] == token_request[:, None]) & (
        position[None, :] < token_visible[:, None]
    )
    return (jnp.where(allowed[:, None, :], scores, -jnp.inf), flat_rows)


def weighted_rows(scores, row_peak, flat_rows):
    weights = jnp.exp(scores - row_peak[:, :, None]).astype(jnp.bfloat16)
    totals = jnp.sum(weights.astype(jnp.float32), axis=2)
    summed = jnp.einsum(
        "thk,kc->thc", weights, flat_rows[:, :LATENT], preferred_element_type=jnp.float32
    )
    return (summed, totals)


def expert_block(arrived, gate_weight, up_weight, down_weight):
    gate_vals = jnp.einsum("prd,pdf->prf", arrived, gate_weight, preferred_element_type=jnp.float32)
    up_vals = jnp.einsum("prd,pdf->prf", arrived, up_weight, preferred_element_type=jnp.float32)
    activated = (jax.nn.silu(gate_vals) * up_vals).astype(jnp.bfloat16)
    return jnp.einsum(
        "prf,pfd->prd", activated, down_weight, preferred_element_type=jnp.float32
    ).astype(jnp.bfloat16)


def body(
    queries,
    latent_cache,
    residual,
    token_request,
    token_visible,
    value_proj,
    out_proj,
    norm_gain,
    router,
    expert_ids,
    gate_weight,
    up_weight,
    down_weight,
):
    all_rows = lax.all_gather(latent_cache, "tp", axis=1, tiled=True)
    scores, flat_rows = masked_scores(queries, all_rows, token_request, token_visible)
    summed, totals = weighted_rows(scores, jnp.max(scores, axis=2), flat_rows)
    context = (summed / totals[:, :, None]).astype(jnp.bfloat16)
    tokens_here = context.shape[0]
    heads_here = context.shape[1]
    head_values = jnp.einsum(
        "thl,hlv->thv",
        context,
        lax.all_gather(value_proj, "ep", axis=1, tiled=True),
        preferred_element_type=jnp.float32,
    )
    heads_out = head_values.astype(jnp.bfloat16).reshape(tokens_here, heads_here * VDIM)
    column_block = jnp.dot(
        lax.all_gather(heads_out, "ep", axis=0, tiled=True),
        out_proj,
        preferred_element_type=jnp.float32,
    )
    attention_part = lax.all_to_all(column_block, "ep", split_axis=0, concat_axis=1, tiled=True)
    attention = lax.psum(attention_part, "tp")
    hidden = (residual.astype(jnp.float32) + attention).astype(jnp.bfloat16)
    hidden_wide = hidden.astype(jnp.float32)
    normed = (
        hidden_wide
        * lax.rsqrt(jnp.mean(hidden_wide * hidden_wide, axis=1, keepdims=True) + epsilon)
        * norm_gain
    ).astype(jnp.bfloat16)
    logits = jnp.dot(normed, router, preferred_element_type=jnp.float32)
    gate_share = jax.nn.softmax(jnp.take_along_axis(logits, expert_ids, axis=1), axis=1).astype(
        jnp.bfloat16
    )
    flat_ids = expert_ids.reshape(-1)
    position_id = jnp.arange(flat_ids.shape[0], dtype=jnp.int32)
    earlier = (flat_ids[:, None] == flat_ids[None, :]) & (
        position_id[None, :] < position_id[:, None]
    )
    slot_ids = (flat_ids * CAP + jnp.sum(earlier.astype(jnp.int32), axis=1)).reshape(
        tokens_here, TOPK
    )
    targets = jnp.arange(EXPERTS * CAP, dtype=jnp.int32)
    matches = slot_ids[:, :, None] == targets[None, None, :]
    picker = jnp.any(matches, axis=1).T.astype(jnp.bfloat16)
    model_width = normed.shape[1]
    mixing = jnp.sum(
        jnp.where(matches, gate_share[:, :, None], jnp.zeros((), jnp.bfloat16)), axis=1
    )
    mixing = jnp.broadcast_to(
        mixing.reshape(tokens_here, EXPERTS, 1, CAP), (tokens_here, EXPERTS, GROUPS, CAP)
    ).reshape(tokens_here, PIECES * CAP)
    core_count = lax.axis_size("tp")
    half_width = model_width // core_count
    core_start = lax.axis_index("tp") * half_width
    outgoing = jnp.dot(picker, normed, preferred_element_type=jnp.float32).astype(jnp.bfloat16)
    outgoing = jnp.broadcast_to(
        outgoing.reshape(EXPERTS, 1, CAP, model_width), (EXPERTS, GROUPS, CAP, model_width)
    ).reshape(PIECES, CAP, model_width)
    arrived = lax.all_to_all(outgoing, "ep", split_axis=0, concat_axis=1, tiled=True)
    partial_out = expert_block(arrived, gate_weight, up_weight, down_weight)
    returned = lax.all_to_all(partial_out, "ep", split_axis=1, concat_axis=0, tiled=True)
    routed = jnp.dot(
        mixing, returned.reshape(PIECES * CAP, model_width), preferred_element_type=jnp.float32
    )
    expert_out = lax.psum_scatter(
        routed.astype(jnp.bfloat16), "tp", scatter_dimension=1, tiled=True
    )
    hidden_part = lax.dynamic_slice_in_dim(hidden, core_start, half_width, 1)
    return (hidden_part, expert_out)


def ring_position(index, count):
    half = lax.div(index, 2)
    return half + lax.rem(index, 2) * (count - 1 - 2 * half)


def ring_index(place, count):
    place = lax.rem(place + count, count)
    upper = lax.div(place, count // 2)
    return 2 * place + upper * (2 * count - 1 - 4 * place)


def greet(count):
    me = lax.axis_index("ep")
    core = lax.axis_index("tp")
    barrier = pltpu.get_barrier_semaphore()
    for step in range(1, count):
        pl.semaphore_signal(
            barrier, inc=1, device_id={"ep": lax.rem(me + step, count)}, device_id_type=MESH
        )
    pl.semaphore_signal(barrier, inc=1, device_id={"tp": 1 - core}, device_id_type=MESH)
    pl.semaphore_wait(barrier, count)


def remote(src, dst, send_sem, recv_sem, where):
    return pltpu.make_async_remote_copy(
        src_ref=src,
        dst_ref=dst,
        send_sem=send_sem,
        recv_sem=recv_sem,
        device_id=where,
        device_id_type=MESH,
    )


def ring_gather(count, own, slot, send_sem, recv_sem, arrived):
    me = lax.axis_index("ep")
    place = ring_position(me, count)
    far = count // 2
    near = count - 1 - far
    to = (ring_index(place + 1, count), ring_index(place - 1, count))

    def reach(way, part):
        return far if way == part else near

    def origin(way, step):
        return ring_index(place - step if way == 0 else place + step, count)

    hops = {}

    def hop(way, step, part):
        if step > reach(way, part):
            return
        block = origin(way, step - 1)
        hops[way, step, part] = remote(
            own(part) if step == 1 else slot(block, part),
            slot(block, part),
            send_sem.at[way, step - 1, part],
            recv_sem.at[way, step - 1, part],
            {"ep": to[way]},
        )
        hops[way, step, part].start()

    for turn in range(2):
        for way in range(2):
            hop(way, 1, (way + turn) % 2)
    arrived(me, 0)
    number = 1
    for step in range(1, far + 1):
        for turn in range(2):
            for way in range(2):
                part = (way + turn) % 2
                if step <= reach(way, part):
                    hops[way, step, part].wait_recv()
                    hop(way, step + 1, part)
        for way in range(2 if step <= near else 1):
            arrived(origin(way, step), number)
            number += 1
    for copy in hops.values():
        copy.wait_send()


def gather_kernel(
    count, cache_ref, value_ref, ids_ref, rows_ref, values_ref, all_ids_ref,
    tp_send, tp_recv, ring_send, ring_recv, id_send, id_recv, own_sem,
):
    me = lax.axis_index("ep")
    core = lax.axis_index("tp")
    some = value_ref.shape[0] // 2
    greet(count)
    swap = remote(cache_ref, rows_ref.at[:, core], tp_send, tp_recv, {"tp": 1 - core})
    swap.start()
    owns = [
        pltpu.make_async_copy(cache_ref, rows_ref.at[:, core], own_sem.at[0]),
        pltpu.make_async_copy(value_ref, values_ref.at[:, me], own_sem.at[1]),
        pltpu.make_async_copy(ids_ref, all_ids_ref.at[me], own_sem.at[2]),
    ]
    for copy in owns:
        copy.start()
    id_copies = [
        remote(
            ids_ref, all_ids_ref.at[me], id_send.at[step - 1], id_recv.at[step - 1],
            {"ep": lax.rem(me + step, count)},
        )
        for step in range(1, count)
    ]
    for copy in id_copies:
        copy.start()
    ring_gather(
        count,
        lambda part: value_ref.at[pl.ds(part * some, some)],
        lambda block, part: values_ref.at[pl.ds(part * some, some), block],
        ring_send,
        ring_recv,
        lambda block, number: None,
    )
    for copy in id_copies:
        copy.wait()
    for copy in owns:
        copy.wait()
    swap.wait()


def middle_kernel(
    count, heads_ref, proj_ref, residual_ref, gain_ref, normed_ref, hidden_ref,
    gathered, mine, theirs, outbox, inbox, hidden_own, normed_own,
    ring_send, ring_recv, pair_send, pair_recv, back_send, back_recv,
    ring2_send, ring2_recv, fwd_send, fwd_recv, own_sem, swap_send, swap_recv,
):
    me = lax.axis_index("ep")
    core = lax.axis_index("tp")
    tokens = heads_ref.shape[0]
    half = tokens // 2
    width = proj_ref.shape[1]
    model = residual_ref.shape[1]
    greet(count)
    pairs = []

    def project(block, number):
        rows = heads_ref[...] if number == 0 else gathered[block]
        product = jnp.dot(rows, proj_ref[...], preferred_element_type=jnp.float32)
        mine[number] = product.reshape(2, half, width)
        copy = remote(
            mine.at[number, 1 - core], theirs.at[number], pair_send.at[number],
            pair_recv.at[number], {"tp": 1 - core},
        )
        copy.start()
        pairs.append((copy, block))

    backs = []

    def pass_back(number):
        copy, block = pairs[number]
        copy.wait_recv()
        total = (mine[number, core] + theirs[number]).astype(jnp.bfloat16)
        if number == 0:
            inbox[me] = total
        else:
            outbox[number - 1] = total
            back = remote(
                outbox.at[number - 1], inbox.at[me], back_send.at[number - 1],
                back_recv.at[number - 1], {"ep": block},
            )
            back.start()
            backs.append(back)

    def arrived(block, number):
        project(block, number)
        if number >= 1:
            pass_back(number - 1)

    ring_gather(
        count,
        lambda part: heads_ref.at[pl.ds(part * half, half)],
        lambda block, part: gathered.at[block, pl.ds(part * half, half)],
        ring_send,
        ring_recv,
        arrived,
    )
    pass_back(count - 1)
    for copy, _ in pairs:
        copy.wait_send()
    for back in backs:
        back.wait()
    attention = jnp.concatenate([inbox[i] for i in range(count)], axis=1).astype(jnp.float32)
    hidden = (residual_ref[...].astype(jnp.float32) + attention).astype(jnp.bfloat16)
    wide = hidden.astype(jnp.float32)
    scale = lax.rsqrt(jnp.mean(wide * wide, axis=1, keepdims=True) + epsilon)
    normed_own[...] = (wide * scale * gain_ref[...]).astype(jnp.bfloat16)
    hidden_own[0] = hidden[:, : model // 2]
    hidden_own[1] = hidden[:, model // 2 :]
    swap = remote(
        hidden_own.at[1 - core], hidden_ref.at[core], swap_send, swap_recv, {"tp": 1 - core}
    )
    swap.start()
    owns = [
        pltpu.make_async_copy(hidden_own.at[core], hidden_ref.at[core], own_sem.at[0]),
        pltpu.make_async_copy(normed_own, normed_ref.at[me, core], own_sem.at[1]),
    ]
    for copy in owns:
        copy.start()
    forwards = []

    def forward(block, number):
        source = normed_own if number == 0 else normed_ref.at[block, core]
        copy = remote(
            source, normed_ref.at[block, core], fwd_send.at[number], fwd_recv.at[number],
            {"tp": 1 - core},
        )
        copy.start()
        forwards.append(copy)

    some = half // 2
    ring_gather(
        count,
        lambda part: normed_own.at[pl.ds(part * some, some)],
        lambda block, part: normed_ref.at[block, core, pl.ds(part * some, some)],
        ring2_send,
        ring2_recv,
        forward,
    )
    for copy in forwards:
        copy.wait()
    for copy in owns:
        copy.wait()
    swap.wait()


def return_kernel(
    count, sums_ref, out_ref, theirs, outbox, inbox, outbox2, inbox2,
    pair_send, pair_recv, cross_send, cross_recv, back_send, back_recv,
):
    me = lax.axis_index("ep")
    core = lax.axis_index("tp")
    half = count // 2
    twin = me + 1 - 2 * lax.rem(me, 2)
    greet(count)
    steps = list(range(1, half)) + [0]
    order = [lax.rem(start + 2 * step, count) for start in (twin, me) for step in steps]
    pairs = []
    for number, block in enumerate(order):
        copy = remote(
            sums_ref.at[1 - core, block], theirs.at[number], pair_send.at[number],
            pair_recv.at[number], {"tp": 1 - core},
        )
        copy.start()
        pairs.append(copy)

    def both(number):
        pairs[number].wait_recv()
        return sums_ref[core, order[number]].astype(jnp.float32) + theirs[number].astype(
            jnp.float32
        )

    crosses = []
    for number in range(half):
        outbox[number] = both(number).astype(jnp.bfloat16)
        cross = remote(
            outbox.at[number], inbox.at[number], cross_send.at[number], cross_recv.at[number],
            {"ep": twin},
        )
        cross.start()
        crosses.append(cross)
    backs = []
    for number in range(half):
        total = both(half + number)
        crosses[number].wait_recv()
        total = total + inbox[number].astype(jnp.float32)
        if number < half - 1:
            outbox2[number] = total.astype(jnp.bfloat16)
            back = remote(
                outbox2.at[number], inbox2.at[number], back_send.at[number],
                back_recv.at[number], {"ep": order[half + number]},
            )
            back.start()
            backs.append(back)
    for number, back in enumerate(backs):
        back.wait_recv()
        total = total + inbox2[number].astype(jnp.float32)
    out_ref[...] = total.astype(jnp.bfloat16)
    for copy in pairs + crosses + backs:
        copy.wait_send()


def expert_kernel(blocks, rows_ref, gate_ref, up_ref, down_ref, out_ref):
    rows = rows_ref[0]
    total = None
    for block in range(blocks):
        gate = lax.dot_general(
            rows, gate_ref[block], (((1,), (1,)), ((), ())), preferred_element_type=jnp.float32
        )
        up = lax.dot_general(
            rows, up_ref[block], (((1,), (1,)), ((), ())), preferred_element_type=jnp.float32
        )
        activated = (gate / (1.0 + jnp.exp(-gate)) * up).astype(jnp.bfloat16)
        part = jnp.dot(activated, down_ref[block], preferred_element_type=jnp.float32)
        total = part if total is None else total + part
    out_ref[0] = total.astype(jnp.bfloat16)


def vmem_call(kernel, outs, scratch, ident, *args):
    whole = pl.BlockSpec(memory_space=pltpu.VMEM)
    return pl.pallas_call(
        kernel,
        out_shape=outs,
        in_specs=[whole] * len(args),
        out_specs=jax.tree.map(lambda _: whole, outs),
        scratch_shapes=scratch,
        compiler_params=pltpu.CompilerParams(
            collective_id=ident, has_side_effects=True, vmem_limit_bytes=40 * 2**20
        ),
    )(*args)


def dma(*shape):
    return pltpu.SemaphoreType.DMA(shape)


def lean_body(
    queries,
    latent_cache,
    residual,
    token_request,
    token_visible,
    value_proj,
    out_proj,
    norm_gain,
    router,
    expert_ids,
    gate_weight,
    up_weight,
    down_weight,
):
    count = lax.axis_size("ep")
    core = lax.axis_index("tp")
    me = lax.axis_index("ep")
    tokens, heads = queries.shape[:2]
    half = tokens // 2
    requests, positions, columns = latent_cache.shape
    model = residual.shape[1]
    bf16 = jnp.bfloat16
    shape = jax.ShapeDtypeStruct
    reach = max(1, count // 2)

    id_rows = -(-tokens * TOPK // 1024) * 8
    flat_ids = jnp.pad(expert_ids.reshape(-1), (0, id_rows * 128 - tokens * TOPK))
    rows, values, all_ids = vmem_call(
        functools.partial(gather_kernel, count),
        (
            shape((requests, 2, positions, columns), bf16),
            shape((value_proj.shape[0], count) + value_proj.shape[1:], bf16),
            shape((count, id_rows, 128), jnp.int32),
        ),
        [
            dma(), dma(), dma(2, reach, 2), dma(2, reach, 2), dma(count - 1), dma(count - 1), dma(3),
        ],
        0,
        latent_cache, value_proj, flat_ids.reshape(id_rows, 128),
    )
    scores, flat_rows = masked_scores(
        queries, rows.reshape(requests, 2 * positions, columns), token_request, token_visible
    )
    summed, totals = weighted_rows(scores, jnp.max(scores, axis=2), flat_rows)
    context = (summed / totals[:, :, None]).astype(bf16)
    head_values = jnp.einsum(
        "thl,hlv->thv",
        context,
        values.reshape(heads, LATENT, VDIM),
        preferred_element_type=jnp.float32,
    )
    heads_out = head_values.astype(bf16).reshape(tokens, heads * VDIM)
    width = out_proj.shape[1]
    normed, hidden = vmem_call(
        functools.partial(middle_kernel, count),
        (shape((count, 2, half, model), bf16), shape((2, half, model // 2), bf16)),
        [
            pltpu.VMEM((count, tokens, heads * VDIM), bf16),
            pltpu.VMEM((count, 2, half, width), jnp.float32),
            pltpu.VMEM((count, half, width), jnp.float32),
            pltpu.VMEM((count - 1, half, width), bf16),
            pltpu.VMEM((count, half, width), bf16),
            pltpu.VMEM((2, half, model // 2), bf16),
            pltpu.VMEM((half, model), bf16),
            dma(2, reach, 2), dma(2, reach, 2), dma(count), dma(count), dma(count - 1), dma(count - 1),
            dma(2, reach, 2), dma(2, reach, 2), dma(count), dma(count), dma(2), dma(), dma(),
        ],
        1,
        heads_out,
        out_proj,
        lax.dynamic_slice_in_dim(residual, core * half, half, 0),
        norm_gain.reshape(1, model),
    )
    normed = normed.reshape(count * tokens, model)

    local = EXPERTS // count
    ids = all_ids.reshape(count, -1)[:, : tokens * TOPK].reshape(count * tokens, TOPK)
    named = jnp.any(ids[:, :, None] == jnp.arange(EXPERTS, dtype=jnp.int32), axis=1)
    logits = jnp.dot(normed, router, preferred_element_type=jnp.float32)
    logits = jnp.where(named, logits, -jnp.inf)
    raised = jnp.exp(logits - jnp.max(logits, axis=1, keepdims=True))
    share = (raised / jnp.sum(raised, axis=1, keepdims=True)).astype(bf16)
    first = me * local
    here = lax.dynamic_slice_in_dim(named, first, local, 1)
    share_here = lax.dynamic_slice_in_dim(share, first, local, 1)
    before = jnp.tril(jnp.ones((tokens, tokens), bf16), -1)
    ranks = jnp.einsum(
        "st,bte->bse",
        before,
        here.reshape(count, tokens, local).astype(bf16),
        preferred_element_type=jnp.float32,
    ).astype(jnp.int32)
    source = jnp.arange(count, dtype=jnp.int32)
    place = (ranks + source[:, None, None] * CAP).reshape(count * tokens, local)
    hits = here[:, :, None] & (place[:, :, None] == jnp.arange(count * CAP, dtype=jnp.int32))
    mixing = jnp.where(hits, share_here[:, :, None], jnp.zeros((), bf16))
    picked = jnp.einsum(
        "tes,td->esd", hits.astype(bf16), normed, preferred_element_type=jnp.float32
    ).astype(bf16)

    slots = count * CAP
    blocks = gate_weight.shape[0] // local
    hidden_here = gate_weight.shape[2]
    expert_rows = pl.pallas_call(
        functools.partial(expert_kernel, blocks),
        grid=(local,),
        out_shape=shape((local, slots, model), bf16),
        in_specs=[
            pl.BlockSpec((1, slots, model), lambda e: (e, 0, 0)),
            pl.BlockSpec((blocks, hidden_here, model), lambda e: (e, 0, 0)),
            pl.BlockSpec((blocks, hidden_here, model), lambda e: (e, 0, 0)),
            pl.BlockSpec((blocks, hidden_here, model), lambda e: (e, 0, 0)),
        ],
        out_specs=pl.BlockSpec((1, slots, model), lambda e: (e, 0, 0)),
        compiler_params=pltpu.CompilerParams(vmem_limit_bytes=40 * 2**20),
    )(picked, jnp.swapaxes(gate_weight, 1, 2), jnp.swapaxes(up_weight, 1, 2), down_weight)
    sums = [
        jnp.einsum(
            "tes,esd->td",
            mixing,
            expert_rows[:, :, side * (model // 2) : (side + 1) * (model // 2)],
            preferred_element_type=jnp.float32,
        ).astype(bf16)
        for side in range(2)
    ]
    sums = jnp.stack(sums).reshape(2, count, tokens, model // 2)
    block = (tokens, model // 2)
    expert_out = vmem_call(
        functools.partial(return_kernel, count),
        shape(block, bf16),
        [
            pltpu.VMEM((count,) + block, bf16),
            pltpu.VMEM((reach,) + block, bf16),
            pltpu.VMEM((reach,) + block, bf16),
            pltpu.VMEM((reach - 1,) + block, bf16),
            pltpu.VMEM((reach - 1,) + block, bf16),
            dma(count), dma(count), dma(reach), dma(reach), dma(reach - 1), dma(reach - 1),
        ],
        2,
        sums,
    )
    return (hidden.reshape(tokens, model // 2), expert_out)


LEAN_BYTES = 8 * 2**20


def choose(mesh):
    count = mesh.shape["ep"]

    def layer(*args):
        tokens, model = args[2].shape
        fits = count * tokens * model * 2 <= LEAN_BYTES
        even = count % 2 == 0 and count >= 4 and tokens % 32 == 0 and EXPERTS % count == 0
        if fits and even and mesh.shape["tp"] == 2:
            return lean_body(*args)
        return body(*args)

    return layer


def solution(mesh):
    return jax.shard_map(
        choose(mesh),
        mesh=mesh,
        in_specs=(
            P(("grp", "ep"), "tp", None),
            P(("grp", "ep"), "tp", None),
            P(("grp", "ep"), None),
            P(("grp", "ep")),
            P(("grp", "ep")),
            P("tp", "ep", None),
            P("tp", "ep"),
            P(),
            P(),
            P(("grp", "ep"), None),
            P("ep", None, "tp"),
            P("ep", None, "tp"),
            P("ep", "tp", None),
        ),
        out_specs=(P(("grp", "ep"), "tp"), P(("grp", "ep"), "tp")),
        check_vma=False,
    )
```

profile of v0, /device:TPU:0, one launch (start us, length us, event | category | flops | bytes accessed | tf_op | source)
XLA Modules:
  0.0 121.8 jit_solution(3834780633240102613)
XLA Ops:
  0.6 0.0 copy-start
  0.6 0.0 copy-start.9
  0.7 0.0 copy-start.8
  0.7 1.6 %copy.27.cache_ref = bf16[3,256,576]{2,1,0:T(8,128)(2,1)S(1)} copy(bf16[3,256,576]{1,2,0:T(8,128)(2,1)} %param.14) | data formatting | bytes 1769472 | tf_op args[1]
  2.3 0.8 copy.26
  3.0 0.1 reshape.118
  3.2 0.0 copy-start.2
  3.2 0.9 copy-done.2
  4.1 21.2 %shard_map.140 = (bf16[3,2,256,576]{3,2,1,0:T(8,128)(2,1)S(1)}, bf16[8,8,64,128]{3,2,1,0:T(8,128)(2,1)S(1)}, s32[8,8,128]{2,1,0:T(8,128)S(1)}) custom-call(bf16[3,256,576]{2,1,0:T(8,128)(2,1)S(1)} %copy.27.cache_ref, bf16[8,64,128]{2,1,0:T(8,128)(2,1)S(1)} %copy-done.2, s32[8,128]{1,0:T(8,128)S(1)} %pad_bitcast_fusion.ids_ref), custom_call_target="tpu_custom_call" | custom-call | tf_op jit(solution)/shard_map/pallas_call | solution.py:443
  25.3 0.0 copy-start.3
  25.3 0.6 copy-done.3
  25.9 0.0 copy-start.5
  25.9 1.3 %copy-done.5 = bf16[3,2,256,576]{3,2,1,0:T(8,128)(2,1)} copy-done((bf16[3,2,256,576]{3,2,1,0:T(8,128)(2,1)}, bf16[3,2,256,576]{3,2,1,0:T(8,128)(2,1)S(1)}, u32[]{:S(2)}) %copy-start.5) | copy-done | bytes 1769496
  27.2 0.0 copy-start.7
  27.2 1.0 copy-done.7
  28.2 0.0 copy-done.9
  28.2 0.0 copy-done.8
  28.2 0.1 compare_and_fusion
  28.4 0.0 copy-done
  28.4 0.0 copy-start.6
  28.4 4.8 %convert_reduce_fusion = (f32[64,8]{0,1:T(8,128)S(1)}, bf16[64,8,1536]{2,0,1:T(8,128)(2,1)}) fusion(bf16[1536,576,1]{1,0,2:T(8,128)(2,1)} %bitcast.65, pred[64,1536]{1,0:T(8,128)(4,1)S(1)} %compare_and_fusion, bf16[64,8,576]{2,1,0:T(8,128)(2,1)S(1)} %copy-done), kind=kOutput, calls=%fused_computation.3 | convolution fusion | flops 910689792 | bytes 4032512 | tf_op jit(solution)/shard_map/sub | solution.py:41
  33.2 0.0 copy-done.6
  33.2 0.0 copy-start.1
  33.2 0.0 copy-start.4
  33.2 2.9 %fusion.4 = bf16[8,8,8,128]{3,2,1,0:T(8,128)(2,1)S(1)} fusion(bf16[8,512,128]{2,1,0:T(8,128)(2,1)} %bitcast.67, bf16[64,8,1536]{2,0,1:T(8,128)(2,1)} %get-tuple-element.15, bf16[1536,576]{1,0:T(8,128)(2,1)S(1)} %bitcast.66, f32[64,8]{0,1:T(8,128)S(1)} %get-tuple-element.14), kind=kOutput, calls=%fused_computation.14 | convolution fusion | flops 873005056 | bytes 4329472 | tf_op jit(solution)/shard_map/thl,hlv->thv/dot_general | solution.py:505
  36.1 0.9 constant_dynamic-slice_fusion.1.residual_ref
  37.0 0.0 copy-done.1
  37.0 0.0 copy-done.4
  37.1 38.2 %shard_map.141 = (bf16[8,2,32,2048]{3,2,1,0:T(8,128)(2,1)S(1)}, bf16[2,32,1024]{2,1,0:T(8,128)(2,1)S(1)}) custom-call(bf16[64,1024]{1,0:T(8,128)(2,1)S(1)} %bitcast.61, bf16[1024,256]{1,0:T(8,128)(2,1)S(1)} %copy-done.1, bf16[32,2048]{1,0:T(8,128)(2,1)S(1)} %constant_dynamic-slice_fusion.1.residual_ref, f32[1,2048]{1,0:T(1,128)S(1)} %bitcast.64), custom_call_target="tpu_custom_call" | custom-call | tf_op jit(solution)/shard_map/pallas_call | solution.py:443
  75.3 0.8 copy.47
  76.1 0.2 eq.52
  76.3 0.1 copy.31
  76.4 0.1 fusion.14
  76.5 1.7 %fusion.49 = (f32[512]{0:T(512)S(1)}, f32[512,64]{0,1:T(8,128)S(1)}) fusion(pred[512,64]{0,1:T(8,128)(4,1)S(1)} %fusion.14, bf16[512,2048]{1,0:T(8,128)(2,1)S(1)} %bitcast.59, bf16[2048,64]{0,1:T(8,128)(2,1)} %param.21), kind=kOutput, calls=%fused_computation.73 | convolution fusion | flops 134282752 | bytes 2525184 | tf_op jit(solution)/shard_map/dot_general | solution.py:538
  78.3 0.1 reshape.125
  78.4 0.2 fusion.6
  78.7 0.1 eq.56
  78.7 1.3 %convolution_convert_fusion.rows_ref = bf16[8,64,2048]{2,1,0:T(8,128)(2,1)S(1)} fusion(bf16[512,2048,1]{1,0,2:T(8,128)(2,1)S(1)} %bitcast.60, s32[512,8]{0,1:T(8,128)S(1)} %eq.56, pred[512,8]{0,1:T(8,128)(4,1)S(1)} %constant_dynamic-slice_fusion), kind=kOutput, calls=%fused_computation.5 | convolution fusion | flops 1075314688 | bytes 4214784 | tf_op jit(solution)/shard_map/tes,td->esd/dot_general | solution.py:556
  80.0 17.5 %shard_map.142 = bf16[8,64,2048]{2,1,0:T(8,128)(2,1)S(1)} custom-call(bf16[8,64,2048]{2,1,0:T(8,128)(2,1)S(1)} %convolution_convert_fusion.rows_ref, bf16[16,192,2048]{2,1,0:T(8,128)(2,1)} %bitcast.68, bf16[16,192,2048]{2,1,0:T(8,128)(2,1)} %bitcast.69, bf16[16,192,2048]{2,1,0:T(8,128)(2,1)} %down_ref.1), custom_call_target="tpu_custom_call" | custom-call | tf_op jit(solution)/shard_map/pallas_call | solution.py:563
  97.5 0.8 bitcast_convert_fusion.1
  98.2 0.8 bitcast_convert_fusion
  99.0 0.2 pad_maximum_fusion.sums_ref
  99.2 21.3 %shard_map.143 = bf16[64,1024]{1,0:T(8,128)(2,1)S(1)} custom-call(bf16[2,8,64,1024]{3,2,1,0:T(8,128)(2,1)S(1)} %pad_maximum_fusion.sums_ref), custom_call_target="tpu_custom_call" | custom-call | tf_op jit(solution)/shard_map/pallas_call | solution.py:443
  120.5 0.7 copy.50
  121.1 0.7 copy.51
  (10 shorter events, 0.1 us)
Async XLA Ops:
  0.6 27.7 %copy-start = (bf16[64,8,576]{2,1,0:T(8,128)(2,1)S(1)}, bf16[64,8,576]{2,1,0:T(8,128)(2,1)}, u32[]{:S(2)}) copy-start(bf16[64,8,576]{2,1,0:T(8,128)(2,1)} %param.13) | copy-start | bytes 1769476
  0.6 27.6 %copy-start.9 = (s32[64]{0:T(128)S(1)}, s32[64]{0:T(128)}, u32[]{:S(2)}) copy-start(s32[64]{0:T(128)} %param.16) | copy-start | bytes 772
  0.7 27.6 %copy-start.8 = (s32[64]{0:T(128)S(1)}, s32[64]{0:T(128)}, u32[]{:S(2)}) copy-start(s32[64]{0:T(128)} %param.17) | copy-start | bytes 772
  3.2 0.9 copy-start.2
  25.3 0.6 copy-start.3
  25.9 1.3 %copy-start.5 = (bf16[3,2,256,576]{3,2,1,0:T(8,128)(2,1)}, bf16[3,2,256,576]{3,2,1,0:T(8,128)(2,1)S(1)}, u32[]{:S(2)}) copy-start(bf16[3,2,256,576]{3,2,1,0:T(8,128)(2,1)S(1)} %get-tuple-element.8) | copy-start | bytes 5308420
  27.2 1.0 copy-start.7
  28.4 4.8 %copy-start.6 = (bf16[3,2,256,576]{3,2,1,0:T(8,128)(2,1)S(1)}, bf16[3,2,256,576]{3,2,1,0:T(8,128)(2,1)}, u32[]{:S(2)}) copy-start(bf16[3,2,256,576]{3,2,1,0:T(8,128)(2,1)} %copy-done.5) | copy-start | bytes 5308420
  33.2 3.8 %copy-start.1 = (bf16[1024,256]{1,0:T(8,128)(2,1)S(1)}, bf16[1024,256]{1,0:T(8,128)(2,1)}, u32[]{:S(2)}) copy-start(bf16[1024,256]{1,0:T(8,128)(2,1)} %proj_ref.1) | copy-start | bytes 1572868
  33.2 3.9 %copy-start.4 = (f32[2048]{0:T(1024)S(1)}, f32[2048]{0:T(1024)}, u32[]{:S(2)}) copy-start(f32[2048]{0:T(1024)} %param.20) | copy-start | bytes 24580
where the time goes:
time: 122 us
  Pallas kernels  98.2 us (80%)
  matrix products  12.4 us (10%)
  local copies, waits for them, and re-layouts  9.83 us (8%)
    pallas_call x3, Pallas kernels, vmem_call(): pl.pallas_call(kernel, out_shape=outs, in_specs=[whole] * len(args), out_...  80.7 us
    pallas_call x1, Pallas kernels, lean_body(): pl.pallas_call(functools.partial(expert_kernel, blocks), grid=(local,), o...  17.5 us
    unnamed x25, local copies, waits for them, and re-layouts  8.24 us
    sub x1, matrix products, weighted_rows(): weights = jnp.exp(scores - row_peak[:, :, None]).astype(jnp.bfloat16)  4.81 us
    dot_general x1, matrix products, lean_body(): jnp.einsum('thl,hlv->thv', context, values.reshape(heads, LATENT, VDIM),...  2.87 us

commit v1 on v0

v1 whole, which is shorter than its diff:
```python
import functools

import jax
import jax.numpy as jnp
from jax import lax
from jax.experimental import pallas as pl
from jax.experimental.pallas import tpu as pltpu
from jax.sharding import PartitionSpec as P

LATENT = 512
VDIM = 128
EXPERTS = 64
TOPK = 6
GROUPS = 2
CAP = 8
PIECES = 128
MESH = pl.DeviceIdType.MESH


score_scale = 192.0 ** (-0.5)
epsilon = 1e-06


def masked_scores(queries, block_rows, token_request, token_visible):
    per_request = block_rows.shape[1]
    flat_rows = block_rows.reshape(-1, block_rows.shape[2])
    scores = (
        jnp.einsum("thc,kc->thk", queries, flat_rows, preferred_element_type=jnp.float32)
        * score_scale
    )
    column = jnp.arange(flat_rows.shape[0], dtype=jnp.int32)
    owner_id = column // per_request
    position = column % per_request
    allowed = (owner_id[None, :] == token_request[:, None]) & (
        position[None, :] < token_visible[:, None]
    )
    return (jnp.where(allowed[:, None, :], scores, -jnp.inf), flat_rows)


def weighted_rows(scores, row_peak, flat_rows):
    weights = jnp.exp(scores - row_peak[:, :, None]).astype(jnp.bfloat16)
    totals = jnp.sum(weights.astype(jnp.float32), axis=2)
    summed = jnp.einsum(
        "thk,kc->thc", weights, flat_rows[:, :LATENT], preferred_element_type=jnp.float32
    )
    return (summed, totals)


def expert_block(arrived, gate_weight, up_weight, down_weight):
    gate_vals = jnp.einsum("prd,pdf->prf", arrived, gate_weight, preferred_element_type=jnp.float32)
    up_vals = jnp.einsum("prd,pdf->prf", arrived, up_weight, preferred_element_type=jnp.float32)
    activated = (jax.nn.silu(gate_vals) * up_vals).astype(jnp.bfloat16)
    return jnp.einsum(
        "prf,pfd->prd", activated, down_weight, preferred_element_type=jnp.float32
    ).astype(jnp.bfloat16)


def body(
    queries,
    latent_cache,
    residual,
    token_request,
    token_visible,
    value_proj,
    out_proj,
    norm_gain,
    router,
    expert_ids,
    gate_weight,
    up_weight,
    down_weight,
):
    all_rows = lax.all_gather(latent_cache, "tp", axis=1, tiled=True)
    scores, flat_rows = masked_scores(queries, all_rows, token_request, token_visible)
    summed, totals = weighted_rows(scores, jnp.max(scores, axis=2), flat_rows)
    context = (summed / totals[:, :, None]).astype(jnp.bfloat16)
    tokens_here = context.shape[0]
    heads_here = context.shape[1]
    head_values = jnp.einsum(
        "thl,hlv->thv",
        context,
        lax.all_gather(value_proj, "ep", axis=1, tiled=True),
        preferred_element_type=jnp.float32,
    )
    heads_out = head_values.astype(jnp.bfloat16).reshape(tokens_here, heads_here * VDIM)
    column_block = jnp.dot(
        lax.all_gather(heads_out, "ep", axis=0, tiled=True),
        out_proj,
        preferred_element_type=jnp.float32,
    )
    attention_part = lax.all_to_all(column_block, "ep", split_axis=0, concat_axis=1, tiled=True)
    attention = lax.psum(attention_part, "tp")
    hidden = (residual.astype(jnp.float32) + attention).astype(jnp.bfloat16)
    hidden_wide = hidden.astype(jnp.float32)
    normed = (
        hidden_wide
        * lax.rsqrt(jnp.mean(hidden_wide * hidden_wide, axis=1, keepdims=True) + epsilon)
        * norm_gain
    ).astype(jnp.bfloat16)
    logits = jnp.dot(normed, router, preferred_element_type=jnp.float32)
    gate_share = jax.nn.softmax(jnp.take_along_axis(logits, expert_ids, axis=1), axis=1).astype(
        jnp.bfloat16
    )
    flat_ids = expert_ids.reshape(-1)
    position_id = jnp.arange(flat_ids.shape[0], dtype=jnp.int32)
    earlier = (flat_ids[:, None] == flat_ids[None, :]) & (
        position_id[None, :] < position_id[:, None]
    )
    slot_ids = (flat_ids * CAP + jnp.sum(earlier.astype(jnp.int32), axis=1)).reshape(
        tokens_here, TOPK
    )
    targets = jnp.arange(EXPERTS * CAP, dtype=jnp.int32)
    matches = slot_ids[:, :, None] == targets[None, None, :]
    picker = jnp.any(matches, axis=1).T.astype(jnp.bfloat16)
    model_width = normed.shape[1]
    mixing = jnp.sum(
        jnp.where(matches, gate_share[:, :, None], jnp.zeros((), jnp.bfloat16)), axis=1
    )
    mixing = jnp.broadcast_to(
        mixing.reshape(tokens_here, EXPERTS, 1, CAP), (tokens_here, EXPERTS, GROUPS, CAP)
    ).reshape(tokens_here, PIECES * CAP)
    core_count = lax.axis_size("tp")
    half_width = model_width // core_count
    core_start = lax.axis_index("tp") * half_width
    outgoing = jnp.dot(picker, normed, preferred_element_type=jnp.float32).astype(jnp.bfloat16)
    outgoing = jnp.broadcast_to(
        outgoing.reshape(EXPERTS, 1, CAP, model_width), (EXPERTS, GROUPS, CAP, model_width)
    ).reshape(PIECES, CAP, model_width)
    arrived = lax.all_to_all(outgoing, "ep", split_axis=0, concat_axis=1, tiled=True)
    partial_out = expert_block(arrived, gate_weight, up_weight, down_weight)
    returned = lax.all_to_all(partial_out, "ep", split_axis=1, concat_axis=0, tiled=True)
    routed = jnp.dot(
        mixing, returned.reshape(PIECES * CAP, model_width), preferred_element_type=jnp.float32
    )
    expert_out = lax.psum_scatter(
        routed.astype(jnp.bfloat16), "tp", scatter_dimension=1, tiled=True
    )
    hidden_part = lax.dynamic_slice_in_dim(hidden, core_start, half_width, 1)
    return (hidden_part, expert_out)


def ring_position(index, count):
    half = lax.div(index, 2)
    return half + lax.rem(index, 2) * (count - 1 - 2 * half)


def ring_index(place, count):
    place = lax.rem(place + count, count)
    upper = lax.div(place, count // 2)
    return 2 * place + upper * (2 * count - 1 - 4 * place)


def greet(count):
    me = lax.axis_index("ep")
    core = lax.axis_index("tp")
    barrier = pltpu.get_barrier_semaphore()
    for step in range(1, count):
        pl.semaphore_signal(
            barrier, inc=1, device_id={"ep": lax.rem(me + step, count)}, device_id_type=MESH
        )
    pl.semaphore_signal(barrier, inc=1, device_id={"tp": 1 - core}, device_id_type=MESH)
    pl.semaphore_wait(barrier, count)


def remote(src, dst, send_sem, recv_sem, where):
    return pltpu.make_async_remote_copy(
        src_ref=src,
        dst_ref=dst,
        send_sem=send_sem,
        recv_sem=recv_sem,
        device_id=where,
        device_id_type=MESH,
    )


def copy_here(src, dst, sem):
    copy = pltpu.make_async_copy(src, dst, sem)
    copy.start()
    return copy


class Ring:
    def __init__(self, count, own, slot, send_sem, recv_sem):
        self.count = count
        self.place = ring_position(lax.axis_index("ep"), count)
        self.far = count // 2
        self.near = count - 1 - self.far
        self.to = (ring_index(self.place + 1, count), ring_index(self.place - 1, count))
        self.own, self.slot = own, slot
        self.send_sem, self.recv_sem = send_sem, recv_sem
        self.hops = {}

    def reach(self, way, part):
        return self.far if way == part else self.near

    def origin(self, way, step):
        return ring_index(self.place - step if way == 0 else self.place + step, self.count)

    def hop(self, way, step, part):
        if step > self.reach(way, part):
            return
        block = self.origin(way, step - 1)
        self.hops[way, step, part] = remote(
            self.own(part) if step == 1 else self.slot(block, part),
            self.slot(block, part),
            self.send_sem.at[way, step - 1, part],
            self.recv_sem.at[way, step - 1, part],
            {"ep": self.to[way]},
        )
        self.hops[way, step, part].start()

    def launch(self):
        for turn in range(2):
            for way in range(2):
                self.hop(way, 1, (way + turn) % 2)

    def relay(self, step):
        for turn in range(2):
            for way in range(2):
                part = (way + turn) % 2
                if step <= self.reach(way, part):
                    self.hops[way, step, part].wait_recv()
                    self.hop(way, step + 1, part)

    def finish(self):
        for copy in self.hops.values():
            copy.wait_send()


def number_of(offset, count):
    far = count // 2
    offset = offset % count
    if offset > far:
        offset -= count
    if offset == 0:
        return 0
    if offset == far:
        return count - 1
    return -2 * offset - 1 if offset < 0 else 2 * offset


def offset_of(number, count):
    if number == count - 1:
        return count // 2
    step = (number + 1) // 2
    return -step if number % 2 else step


class Pieces:
    def __init__(self, count, held, ring_send, ring_recv, side_send, side_recv):
        self.count = count
        self.place = ring_position(lax.axis_index("ep"), count)
        self.core = lax.axis_index("tp")
        self.far = count // 2
        self.near = count - 1 - self.far
        self.to = (ring_index(self.place + 1, count), ring_index(self.place - 1, count))
        self.held = held
        self.sems = (ring_send, ring_recv, side_send, side_recv)
        self.hops, self.sides = {}, {}

    def piece(self, offset, number):
        block = ring_index(self.place + offset + offset_of(number, self.count), self.count)
        return self.held.at[block, ring_index(self.place + offset, self.count), self.core]

    def reach(self, way, number):
        return self.far if number % 2 == way else self.near

    def hop(self, way, step, number):
        if step > self.reach(way, number):
            return
        ref = self.piece(-(step - 1) if way == 0 else step - 1, number)
        copy = remote(
            ref, ref, self.sems[0].at[number, way, step - 1], self.sems[1].at[number, way, step - 1],
            {"ep": self.to[way]},
        )
        copy.start()
        self.hops[way, step, number] = copy

    def side(self, offset, number):
        ref = self.piece(offset, number)
        where = offset % self.count
        copy = remote(
            ref, ref, self.sems[2].at[number, where], self.sems[3].at[number, where],
            {"tp": 1 - self.core},
        )
        copy.start()
        self.sides[where, number] = copy

    def launch(self, number):
        for turn in range(2):
            self.hop((number + turn) % 2, 1, number)
        self.side(0, number)

    def relay(self, step, number):
        for turn in range(2):
            way = (number + turn) % 2
            if step <= self.reach(way, number):
                self.hops[way, step, number].wait_recv()
                self.hop(way, step + 1, number)
                self.side(-step if way == 0 else step, number)

    def settle(self, offset):
        for other in range(self.count):
            self.sides[other, number_of(offset - other, self.count)].wait_recv()

    def finish(self):
        for copy in list(self.hops.values()) + list(self.sides.values()):
            copy.wait_send()


def group_of(step, count):
    far = count // 2
    if step == 0:
        return [0]
    if step == far:
        return [count - 1]
    return [2 * step - 1, 2 * step]


ROWS = 256


def layer_kernel(
    count, meta_ref, gain_ref, queries_hbm, cache_hbm, value_hbm, proj_hbm, residual_hbm, router_hbm,
    gate_hbm, up_hbm, down_hbm, hidden_ref, out_ref,
    queries, cache, values, proj, residual_own, residual, router, gate, up, down,
    limits, context, heads_own, heads_all, mine, theirs, held, ids_all, local_v, picked, mixing, active,
    rows_v, sums, sums2, outbox, inbox, outbox2, inbox2, totals,
    load_sem, weight_sem, swap_sem, id_send, id_recv, res_send, res_recv,
    value_send, value_recv, heads_send, heads_recv, pair_send, pair_recv,
    piece_send, piece_recv, side_send, side_recv,
    both_send, both_recv, cross_send, cross_recv, back_send, back_recv,
):
    me = lax.axis_index("ep")
    core = lax.axis_index("tp")
    f32, bf16 = jnp.float32, jnp.bfloat16
    heads, _, latent, vdim = values.shape[0], values.shape[1], values.shape[1] * values.shape[2], values.shape[3]
    tokens = heads_own.shape[0]
    model = residual_own.shape[1]
    width = proj.shape[1]
    part = width // 2
    requests, columns, positions = cache.shape[1:]
    local = EXPERTS // count
    blocks = gate.shape[0] // local
    some = heads // 2
    half = tokens // 2
    place = ring_position(me, count)
    far = count // 2

    load_value = copy_here(value_hbm, values.at[:, me], load_sem.at[0])
    load_cache = copy_here(cache_hbm, cache.at[core], load_sem.at[1])
    load_residual = copy_here(residual_hbm, residual_own, load_sem.at[2])
    load_queries = copy_here(queries_hbm, queries, load_sem.at[3])
    load_proj = copy_here(proj_hbm, proj, load_sem.at[4])
    load_router = copy_here(router_hbm, router, load_sem.at[5])
    for number, (source, target) in enumerate(((gate_hbm, gate), (up_hbm, up), (down_hbm, down))):
        for expert in range(local):
            span = pl.ds(expert * blocks, blocks)
            pltpu.make_async_copy(source.at[span], target.at[span], weight_sem.at[number, expert]).start()
    ids_all[me] = meta_ref[...]
    greet(count)

    load_value.wait()
    value_ring = Ring(
        count,
        lambda p: values.at[pl.ds(p * some, some), me],
        lambda block, p: values.at[pl.ds(p * some, some), block],
        value_send, value_recv,
    )
    value_ring.launch()
    load_cache.wait()
    swap = remote(cache.at[core], cache.at[core], swap_sem.at[0], swap_sem.at[1], {"tp": 1 - core})
    swap.start()
    load_residual.wait()
    spreads = []
    for step in range(1, count):
        peer = lax.rem(me + step, count)
        column = pl.multiple_of(peer * width + core * part, part)
        spreads.append(
            remote(
                residual_own.at[:, pl.ds(column, part)], residual.at[me],
                res_send.at[step - 1], res_recv.at[step - 1], {"ep": peer},
            )
        )
        spreads.append(
            remote(
                ids_all.at[me], ids_all.at[me], id_send.at[step - 1], id_recv.at[step - 1], {"ep": peer}
            )
        )
    for copy in spreads:
        copy.start()
    residual[me] = residual_own[:, pl.ds(pl.multiple_of(me * width + core * part, part), part)]

    meta = meta_ref[...]
    visible = meta[TOPK : TOPK + 1, :tokens]
    request = meta[TOPK + 1 : TOPK + 2, :tokens]
    row_token = lax.broadcasted_iota(jnp.int32, (tokens * heads, tokens), 0) // heads
    own_token = row_token == lax.broadcasted_iota(jnp.int32, (tokens * heads, tokens), 1)
    for r in range(requests):
        seen = jnp.where(request == r, visible, 0).astype(f32)
        limits[:, r : r + 1] = jnp.sum(jnp.where(own_token, seen, 0.0), axis=1, keepdims=True)

    def attend(start):
        rows = pl.ds(start, ROWS)
        asked = queries[rows, :]
        lane = lax.broadcasted_iota(jnp.int32, (ROWS, positions), 1).astype(f32)
        scored = []
        peak = None
        for r in range(requests):
            limit = limits[rows, r : r + 1]
            for side in range(2):
                score = jnp.dot(asked, cache[side, r], preferred_element_type=f32) * score_scale
                score = jnp.where(lane + float(side * positions) < limit, score, -jnp.inf)
                scored.append(score)
                top = jnp.max(score, axis=1, keepdims=True)
                peak = top if peak is None else jnp.maximum(peak, top)
        total, summed = None, None
        for number, score in enumerate(scored):
            weight = jnp.exp(score - peak).astype(bf16)
            amount = jnp.sum(weight.astype(f32), axis=1, keepdims=True)
            r, side = number // 2, number % 2
            term = lax.dot_general(
                weight, cache[side, r, :latent, :], (((1,), (1,)), ((), ())), preferred_element_type=f32
            )
            total = amount if total is None else total + amount
            summed = term if summed is None else summed + term
        summed = summed / total
        for piece in range(latent // 128):
            context[piece, rows, :] = summed[:, piece * 128 : (piece + 1) * 128]

    load_queries.wait()
    value_ring.relay(1)
    swap.wait_recv()
    chunks = list(range(0, tokens * heads, ROWS))
    done = 0
    for step in range(2, far + 1):
        until = -(-len(chunks) * (step - 1) // (far - 1)) if step < far else len(chunks)
        for start in chunks[done:until]:
            attend(start)
        done = until
        value_ring.relay(step)
    for h in range(heads):
        rows = jnp.concatenate(
            [context[piece, pl.ds(h, tokens, stride=heads), :] for piece in range(latent // 128)], axis=1
        ).astype(bf16)
        heads_own[:, h * vdim : (h + 1) * vdim] = jnp.dot(
            rows, values[h].reshape(latent, vdim), preferred_element_type=f32
        ).astype(bf16)

    heads_ring = Ring(
        count,
        lambda p: heads_own.at[pl.ds(p * half, half)],
        lambda block, p: heads_all.at[block, pl.ds(p * half, half)],
        heads_send, heads_recv,
    )
    heads_ring.launch()
    load_proj.wait()
    for copy in spreads:
        copy.wait_recv()
    load_router.wait()
    pieces = Pieces(count, held, piece_send, piece_recv, side_send, side_recv)
    pairs = {}

    def block_at(offset):
        return ring_index(place + offset, count)

    def project(number):
        rows = heads_own[...] if number == 0 else heads_all[block_at(offset_of(number, count))]
        product = jnp.dot(rows, proj[...], preferred_element_type=f32)
        mine[number, 0] = product[:, :part]
        mine[number, 1] = product[:, part:]
        copy = remote(
            mine.at[number, 1 - core], theirs.at[number], pair_send.at[number], pair_recv.at[number],
            {"tp": 1 - core},
        )
        copy.start()
        pairs[number] = copy

    def conclude(number):
        pairs[number].wait_recv()
        block = block_at(offset_of(number, count))
        attention = mine[number, core] + theirs[number]
        held[block, me, core] = (residual[block].astype(f32) + attention).astype(bf16)
        pieces.launch(number)

    expert_row = lax.broadcasted_iota(jnp.int32, (EXPERTS, tokens), 0)
    before = (
        lax.broadcasted_iota(jnp.int32, (tokens, tokens), 0)
        < lax.broadcasted_iota(jnp.int32, (tokens, tokens), 1)
    ).astype(bf16)
    slot = lax.broadcasted_iota(jnp.int32, (local, CAP, tokens), 1).astype(f32)

    def route(offset):
        pieces.settle(offset)
        block = block_at(offset)
        index = offset % count
        wide = jnp.concatenate(
            [held[block, e, c] for e in range(count) for c in range(2)], axis=1
        ).astype(f32)
        scale = lax.rsqrt(jnp.mean(wide * wide, axis=1, keepdims=True) + epsilon)
        normed = (wide * scale * gain_ref[...]).astype(bf16)
        logits = lax.dot_general(
            router[...], normed, (((1,), (1,)), ((), ())), preferred_element_type=f32
        )
        ids = ids_all[block][:TOPK, :tokens]
        named = expert_row == ids[0:1]
        for k in range(1, TOPK):
            named = named | (expert_row == ids[k : k + 1])
        logits = jnp.where(named, logits, -jnp.inf)
        raised = jnp.exp(logits - jnp.max(logits, axis=0, keepdims=True))
        share = raised / jnp.sum(raised, axis=0, keepdims=True)
        local_v[0] = named.astype(f32)
        local_v[1] = share
        first = pl.ds(pl.multiple_of(me * local, local), local)
        here = local_v[0, first, :]
        share_here = local_v[1, first, :].astype(bf16).astype(f32)
        rank = jnp.dot(here.astype(bf16), before, preferred_element_type=f32)
        hits = (here[:, None, :] > 0.5) & (rank[:, None, :] == slot)
        mixing[index] = (
            jnp.where(hits, share_here[:, None, :], 0.0).reshape(local * CAP, tokens).astype(bf16)
        )
        chosen = jnp.dot(
            jnp.where(hits, 1.0, 0.0).reshape(local * CAP, tokens).astype(bf16), normed,
            preferred_element_type=f32,
        )
        for e in range(local):
            picked[e, pl.ds(index * CAP, CAP), :] = chosen[e * CAP : (e + 1) * CAP]

    for turn in range(2 * far + 1):
        if 1 <= turn <= far:
            heads_ring.relay(turn)
        if turn <= far:
            for number in group_of(turn, count):
                project(number)
        for group in range(far + 1):
            if 1 <= turn - group <= far:
                for number in group_of(group, count):
                    pieces.relay(turn - group, number)
        if turn <= far:
            for number in group_of(turn, count):
                conclude(number)
        if turn >= far:
            for offset in sorted({2 * far - turn, turn - 2 * far}):
                if offset != -far:
                    route(offset)

    hidden_ref[...] = jnp.concatenate(
        [held[me, (count // 2) * core + e, c] for e in range(count // 2) for c in range(2)], axis=1
    )

    def weights(number, expert):
        span = pl.ds(expert * blocks, blocks)
        source, target = ((gate_hbm, gate), (up_hbm, up), (down_hbm, down))[number]
        return pltpu.make_async_copy(source.at[span], target.at[span], weight_sem.at[number, expert])

    inner = blocks * gate.shape[1]

    def excite(expert, carry):
        weights(0, expert).wait()
        weights(1, expert).wait()
        span = pl.ds(expert * blocks, blocks)
        slots = picked[expert].astype(bf16)
        dims = (((1,), (1,)), ((), ()))
        gate_t = lax.dot_general(gate[span].reshape(inner, model), slots, dims, preferred_element_type=f32)
        up_t = lax.dot_general(up[span].reshape(inner, model), slots, dims, preferred_element_type=f32)
        active_t = gate_t / (1.0 + jnp.exp(-gate_t)) * up_t
        active[expert] = active_t.T.astype(bf16)
        return carry

    lax.fori_loop(0, local, excite, 0)
    for expert in range(local):
        weights(2, expert).wait()

    piece = sums.shape[4]
    turns = sums.shape[0]
    side_width = model // 2
    twin = me + 1 - 2 * lax.rem(me, 2)
    pair = count // 2
    steps = list(range(1, pair)) + [0]
    near_order = [lax.rem(me + 2 * step, count) for step in steps]
    twin_order = [lax.rem(twin + 2 * step, count) for step in steps]
    boths, crosses, backs = {}, {}, {}

    def lower(turn):
        def one(expert, carry):
            span = pl.ds(expert * blocks, blocks)
            for c in range(2):
                column = pl.ds(c * side_width + turn * piece, piece)
                rows_v[expert, :, c * piece : (c + 1) * piece] = jnp.dot(
                    active[expert], down[span, :, column].reshape(inner, piece),
                    preferred_element_type=f32,
                )
            return carry

        lax.fori_loop(0, local, one, 0)
        for offset in range(count):
            rows = jnp.concatenate(
                [rows_v[e, offset * CAP : (offset + 1) * CAP, :] for e in range(local)], axis=0
            ).astype(bf16)
            mixed = lax.dot_general(
                mixing[offset], rows, (((0,), (0,)), ((), ())), preferred_element_type=f32
            ).astype(bf16)
            block = block_at(offset)
            for c in range(2):
                sums[turn, c, block] = mixed[:, c * piece : (c + 1) * piece]
        boths[turn] = remote(
            sums.at[turn, 1 - core], sums2.at[turn], both_send.at[turn], both_recv.at[turn],
            {"tp": 1 - core},
        )
        boths[turn].start()

    def added(turn, block):
        return sums[turn, core, block].astype(f32) + sums2[turn, block].astype(f32)

    def cross(turn):
        boths[turn].wait_recv()
        for i, block in enumerate(twin_order):
            outbox[turn, i] = added(turn, block).astype(bf16)
        crosses[turn] = remote(
            outbox.at[turn], inbox.at[turn], cross_send.at[turn], cross_recv.at[turn], {"ep": twin}
        )
        crosses[turn].start()

    def back(turn):
        crosses[turn].wait_recv()
        for i, block in enumerate(near_order):
            total = added(turn, block) + inbox[turn, i].astype(f32)
            if i == pair - 1:
                totals[turn] = total
                continue
            outbox2[turn, i] = total.astype(bf16)
            backs[turn, i] = remote(
                outbox2.at[turn, i], inbox2.at[turn, i], back_send.at[turn, i], back_recv.at[turn, i],
                {"ep": block},
            )
            backs[turn, i].start()

    def end(turn):
        total = totals[turn]
        for i in range(pair - 1):
            backs[turn, i].wait_recv()
            total = total + inbox2[turn, i].astype(f32)
        out_ref[:, turn * piece : (turn + 1) * piece] = total.astype(bf16)

    for turn in range(turns):
        lower(turn)
        if turn >= 1:
            cross(turn - 1)
    cross(turns - 1)
    for turn in range(turns):
        back(turn)
    for turn in range(turns):
        end(turn)

    value_ring.finish()
    heads_ring.finish()
    pieces.finish()
    swap.wait_send()
    for copy in spreads:
        copy.wait_send()
    for group in (pairs, boths, crosses, backs):
        for copy in group.values():
            copy.wait_send()


def dma(*shape):
    return pltpu.SemaphoreType.DMA(shape)


TURNS = 4


def lean_body(
    queries,
    latent_cache,
    residual,
    token_request,
    token_visible,
    value_proj,
    out_proj,
    norm_gain,
    router,
    expert_ids,
    gate_weight,
    up_weight,
    down_weight,
):
    count = lax.axis_size("ep")
    tokens, heads, columns = queries.shape
    requests, positions, _ = latent_cache.shape
    model = residual.shape[1]
    bf16, f32 = jnp.bfloat16, jnp.float32
    shape = jax.ShapeDtypeStruct
    far = count // 2
    local = EXPERTS // count
    width = out_proj.shape[1]
    slots = count * CAP
    blocks = gate_weight.shape[0] // local
    hidden_here = gate_weight.shape[2]
    piece = model // 2 // TURNS
    meta = jnp.concatenate([expert_ids.T, token_visible[None], token_request[None]], axis=0)
    meta = jnp.pad(meta, ((0, 8 - meta.shape[0]), (0, 128 - tokens)))
    whole = pl.BlockSpec(memory_space=pltpu.VMEM)
    anywhere = pl.BlockSpec(memory_space=pl.ANY)
    vmem = pltpu.VMEM
    weight = (gate_weight.shape[0], hidden_here, model)
    hidden, expert_out = pl.pallas_call(
        functools.partial(layer_kernel, count),
        out_shape=(shape((tokens, model // 2), bf16), shape((tokens, model // 2), bf16)),
        in_specs=[whole] * 2 + [anywhere] * 9,
        out_specs=(whole, whole),
        scratch_shapes=[
            vmem((tokens * heads, columns), bf16),
            vmem((2, requests, columns, positions), bf16),
            vmem((heads, count) + value_proj.shape[1:], bf16),
            vmem(out_proj.shape, bf16),
            vmem((tokens, model), bf16),
            vmem((count, tokens, width // 2), bf16),
            vmem((EXPERTS, model), bf16),
            vmem(weight, bf16),
            vmem(weight, bf16),
            vmem(weight, bf16),
            vmem((tokens * heads, 128), f32),
            vmem((LATENT // 128, tokens * heads, 128), f32),
            vmem((tokens, heads * VDIM), bf16),
            vmem((count, tokens, heads * VDIM), bf16),
            vmem((count, 2, tokens, width // 2), f32),
            vmem((count, tokens, width // 2), f32),
            vmem((count, count, 2, tokens, width // 2), bf16),
            vmem((count, 8, 128), jnp.int32),
            vmem((2, EXPERTS, tokens), f32),
            vmem((local, slots, model), f32),
            vmem((count, local * CAP, tokens), bf16),
            vmem((local, slots, blocks * hidden_here), bf16),
            vmem((local, slots, 2 * piece), f32),
            vmem((TURNS, 2, count, tokens, piece), bf16),
            vmem((TURNS, count, tokens, piece), bf16),
            vmem((TURNS, far, tokens, piece), bf16),
            vmem((TURNS, far, tokens, piece), bf16),
            vmem((TURNS, far - 1, tokens, piece), bf16),
            vmem((TURNS, far - 1, tokens, piece), bf16),
            vmem((TURNS, tokens, piece), f32),
            dma(6), dma(3, local), dma(2), dma(count - 1), dma(count - 1), dma(count - 1), dma(count - 1),
            dma(2, far, 2), dma(2, far, 2), dma(2, far, 2), dma(2, far, 2), dma(count), dma(count),
            dma(count, 2, far), dma(count, 2, far), dma(count, count), dma(count, count),
            dma(TURNS), dma(TURNS), dma(TURNS), dma(TURNS), dma(TURNS, far - 1), dma(TURNS, far - 1),
        ],
        compiler_params=pltpu.CompilerParams(
            collective_id=0, has_side_effects=True, vmem_limit_bytes=63 * 2**20
        ),
    )(
        meta, norm_gain.reshape(1, model), queries.reshape(tokens * heads, columns),
        jnp.swapaxes(latent_cache, 1, 2), value_proj, out_proj, residual, router.T,
        jnp.swapaxes(gate_weight, 1, 2), jnp.swapaxes(up_weight, 1, 2), down_weight,
    )
    return (hidden, expert_out)


LEAN_BYTES = 8 * 2**20


def choose(mesh):
    count = mesh.shape["ep"]

    def layer(*args):
        tokens, model = args[2].shape
        fits = count * tokens * model * 2 <= LEAN_BYTES
        even = count % 2 == 0 and count >= 4 and tokens % 32 == 0 and EXPERTS % count == 0
        if fits and even and mesh.shape["tp"] == 2:
            return lean_body(*args)
        return body(*args)

    return layer


def solution(mesh):
    return jax.shard_map(
        choose(mesh),
        mesh=mesh,
        in_specs=(
            P(("grp", "ep"), "tp", None),
            P(("grp", "ep"), "tp", None),
            P(("grp", "ep"), None),
            P(("grp", "ep")),
            P(("grp", "ep")),
            P("tp", "ep", None),
            P("tp", "ep"),
            P(),
            P(),
            P(("grp", "ep"), None),
            P("ep", None, "tp"),
            P("ep", None, "tp"),
            P("ep", "tp", None),
        ),
        out_specs=(P(("grp", "ep"), "tp"), P(("grp", "ep"), "tp")),
        check_vma=False,
    )
```

time: 122 us -> 101 us (0.83)
  matrix products: 12.4 us -> 0 us
  local copies, waits for them, and re-layouts: 9.83 us -> 3.73 us
  Pallas kernels: 98.2 us -> 96.1 us
    dot_general x6 -> x0, matrix products: 7.55 us -> none  [the longest x1 2.87 us: lean_body(): jnp.einsum('thl,hlv->thv', context, values.reshape(heads, LATENT, VDIM),...]
    unnamed x25 -> x2, local copies, waits for them, and re-layouts: 8.24 us -> 3.14 us
    sub x1 -> x0, matrix products: 4.81 us -> none  [weighted_rows(): weights = jnp.exp(scores - row_peak[:, :, None]).astype(jnp.bfloat16)]
    pallas_call x4 -> x1, Pallas kernels: 98.2 us -> 96.1 us  [lean_body(): pl.pallas_call(functools.partial(layer_kernel, count), out_shape=(shape((...]
where the time goes in v1:
time: 101 us
  Pallas kernels  96.1 us (95%)
  local copies, waits for them, and re-layouts  3.73 us (4%)
    pallas_call x1, Pallas kernels, lean_body(): pl.pallas_call(functools.partial(layer_kernel, count), out_shape=(shape((...  96.1 us
    unnamed x2, local copies, waits for them, and re-layouts  3.14 us

profile of v1, /device:TPU:0, one launch (start us, length us, event | category | flops | bytes accessed | tf_op | source)
XLA Modules:
  0.0 101.2 jit_solution(6738477064600025181)
XLA Ops:
  0.6 0.7 pad_add_fusion
  1.4 0.6 pad.4.meta_ref
  2.0 96.1 %shard_map.140 = (bf16[64,1024]{1,0:T(8,128)(2,1)}, bf16[64,1024]{1,0:T(8,128)(2,1)}) custom-call(s32[8,128]{1,0:T(8,128)} %pad.4.meta_ref, f32[1,2048]{1,0:T(1,128)} %bitcast.14, bf16[512,576]{1,0:T(8,128)(2,1)} %bitcast.12, bf16[3,576,256]{2,1,0:T(8,128)(2,1)} %bitcast.11, bf16[8,64,128]{2,1,0:T(8,128)(2,1)} %value_hbm.1, bf16[1024,256]{1,0:T(8,128)(2,1)} %proj_hbm.1, ...), custom_call_target="tpu_custom_call" | custom-call | tf_op jit(solution)/shard_map/pallas_call | solution.py:707
  98.1 1.6 %copy.17 = bf16[64,1024]{1,0:T(8,128)(2,1)} copy(bf16[64,1024]{1,0:T(8,128)(2,1)} %get-tuple-element.4) | data formatting | bytes 262144
  99.7 1.6 %copy.18 = bf16[64,1024]{1,0:T(8,128)(2,1)} copy(bf16[64,1024]{1,0:T(8,128)(2,1)} %get-tuple-element.5) | data formatting | bytes 262144

commit v2 on v1

--- a/solution.py
+++ b/solution.py
@@ -173,6 +173,10 @@
     )
 
 
+def drain(ref, sem):
+    pltpu.make_async_copy(ref, ref, sem).wait()
+
+
 def copy_here(src, dst, sem):
     copy = pltpu.make_async_copy(src, dst, sem)
     copy.start()
@@ -189,9 +193,16 @@
         self.own, self.slot = own, slot
         self.send_sem, self.recv_sem = send_sem, recv_sem
         self.hops = {}
+        self.order = [
+            (way, part)
+            for turn in range(2)
+            for pair in range(PARTS // 2)
+            for way in range(2)
+            for part in (2 * pair + (way + turn) % 2,)
+        ]
 
     def reach(self, way, part):
-        return self.far if way == part else self.near
+        return self.far if way == part % 2 else self.near
 
     def origin(self, way, step):
         return ring_index(self.place - step if way == 0 else self.place + step, self.count)
@@ -203,29 +214,21 @@
         self.hops[way, step, part] = remote(
             self.own(part) if step == 1 else self.slot(block, part),
             self.slot(block, part),
-            self.send_sem.at[way, step - 1, part],
+            self.send_sem,
             self.recv_sem.at[way, step - 1, part],
             {"ep": self.to[way]},
         )
         self.hops[way, step, part].start()
 
     def launch(self):
-        for turn in range(2):
-            for way in range(2):
-                self.hop(way, 1, (way + turn) % 2)
+        for way, part in self.order:
+            self.hop(way, 1, part)
 
     def relay(self, step):
-        for turn in range(2):
-            for way in range(2):
-                part = (way + turn) % 2
-                if step <= self.reach(way, part):
-                    self.hops[way, step, part].wait_recv()
-                    self.hop(way, step + 1, part)
-
-    def finish(self):
-        for copy in self.hops.values():
-            copy.wait_send()
-
+        for way, part in self.order:
+            if step <= self.reach(way, part):
+                self.hops[way, step, part].wait_recv()
+                self.hop(way, step + 1, part)
 
 def number_of(offset, count):
     far = count // 2
@@ -270,21 +273,15 @@
             return
         ref = self.piece(-(step - 1) if way == 0 else step - 1, number)
         copy = remote(
-            ref, ref, self.sems[0].at[number, way, step - 1], self.sems[1].at[number, way, step - 1],
-            {"ep": self.to[way]},
+            ref, ref, self.sems[0], self.sems[1].at[number, way, step - 1], {"ep": self.to[way]}
         )
         copy.start()
         self.hops[way, step, number] = copy
 
     def side(self, offset, number):
         ref = self.piece(offset, number)
-        where = offset % self.count
-        copy = remote(
-            ref, ref, self.sems[2].at[number, where], self.sems[3].at[number, where],
-            {"tp": 1 - self.core},
-        )
-        copy.start()
-        self.sides[where, number] = copy
+        where = (offset + offset_of(number, self.count)) % self.count
+        remote(ref, ref, self.sems[2], self.sems[3].at[where], {"tp": 1 - self.core}).start()
 
     def launch(self, number):
         for turn in range(2):
@@ -300,12 +297,11 @@
                 self.side(-step if way == 0 else step, number)
 
     def settle(self, offset):
-        for other in range(self.count):
-            self.sides[other, number_of(offset - other, self.count)].wait_recv()
+        drain(self.held.at[0, :, 0], self.sems[3].at[offset % self.count])
 
     def finish(self):
-        for copy in list(self.hops.values()) + list(self.sides.values()):
-            copy.wait_send()
+        drain(self.held.at[: self.count - 1, :, 0], self.sems[0])
+        drain(self.held.at[:, :, 0], self.sems[2])
 
 
 def group_of(step, count):
@@ -318,15 +314,16 @@
 
 
 ROWS = 256
+PARTS = 4
 
 
 def layer_kernel(
-    count, meta_ref, gain_ref, queries_hbm, cache_hbm, value_hbm, proj_hbm, residual_hbm, router_hbm,
+    count, ids_ref, visible_ref, request_ref, gain_ref, queries_hbm, cache_hbm, value_hbm, proj_hbm, residual_hbm, router_hbm,
     gate_hbm, up_hbm, down_hbm, hidden_ref, out_ref,
     queries, cache, values, proj, residual_own, residual, router, gate, up, down,
     limits, context, heads_own, heads_all, mine, theirs, held, ids_all, local_v, picked, mixing, active,
-    rows_v, sums, sums2, outbox, inbox, outbox2, inbox2, totals,
-    load_sem, weight_sem, swap_sem, id_send, id_recv, res_send, res_recv,
+    sums, sums2, outbox, inbox, outbox2, inbox2, totals,
+    load_sem, excite_sem, lower_sem, swap_sem, id_sem, res_sem,
     value_send, value_recv, heads_send, heads_recv, pair_send, pair_recv,
     piece_send, piece_recv, side_send, side_recv,
     both_send, both_recv, cross_send, cross_recv, back_send, back_recv,
@@ -342,8 +339,8 @@
     requests, columns, positions = cache.shape[1:]
     local = EXPERTS // count
     blocks = gate.shape[0] // local
-    some = heads // 2
-    half = tokens // 2
+    some = heads // PARTS
+    half = tokens // PARTS
     place = ring_position(me, count)
     far = count // 2
 
@@ -353,11 +350,7 @@
     load_queries = copy_here(queries_hbm, queries, load_sem.at[3])
     load_proj = copy_here(proj_hbm, proj, load_sem.at[4])
     load_router = copy_here(router_hbm, router, load_sem.at[5])
-    for number, (source, target) in enumerate(((gate_hbm, gate), (up_hbm, up), (down_hbm, down))):
-        for expert in range(local):
-            span = pl.ds(expert * blocks, blocks)
-            pltpu.make_async_copy(source.at[span], target.at[span], weight_sem.at[number, expert]).start()
-    ids_all[me] = meta_ref[...]
+    ids_all[me, :TOPK, :tokens] = ids_ref[...]
     greet(count)
 
     load_value.wait()
@@ -372,28 +365,25 @@
     swap = remote(cache.at[core], cache.at[core], swap_sem.at[0], swap_sem.at[1], {"tp": 1 - core})
     swap.start()
     load_residual.wait()
+    load_queries.wait()
+    load_proj.wait()
+    load_router.wait()
+    for expert in range(local):
+        span = pl.ds(expert * blocks, blocks)
+        for source, target in ((gate_hbm, gate), (up_hbm, up)):
+            pltpu.make_async_copy(source.at[span], target.at[span], excite_sem.at[expert]).start()
+    load_down = copy_here(down_hbm, down, lower_sem)
     spreads = []
     for step in range(1, count):
         peer = lax.rem(me + step, count)
         column = pl.multiple_of(peer * width + core * part, part)
         spreads.append(
-            remote(
-                residual_own.at[:, pl.ds(column, part)], residual.at[me],
-                res_send.at[step - 1], res_recv.at[step - 1], {"ep": peer},
-            )
-        )
-        spreads.append(
-            remote(
-                ids_all.at[me], ids_all.at[me], id_send.at[step - 1], id_recv.at[step - 1], {"ep": peer}
-            )
-        )
-    for copy in spreads:
-        copy.start()
+            remote(residual_own.at[:, pl.ds(column, part)], residual.at[me], res_sem.at[0], res_sem.at[1], {"ep": peer})
+        )
+        spreads.append(remote(ids_all.at[me], ids_all.at[me], id_sem.at[0], id_sem.at[1], {"ep": peer}))
     residual[me] = residual_own[:, pl.ds(pl.multiple_of(me * width + core * part, part), part)]
 
-    meta = meta_ref[...]
-    visible = meta[TOPK : TOPK + 1, :tokens]
-    request = meta[TOPK + 1 : TOPK + 2, :tokens]
+    visible, request = visible_ref[...], request_ref[...]
     row_token = lax.broadcasted_iota(jnp.int32, (tokens * heads, tokens), 0) // heads
     own_token = row_token == lax.broadcasted_iota(jnp.int32, (tokens * heads, tokens), 1)
     for r in range(requests):
@@ -428,7 +418,6 @@
         for piece in range(latent // 128):
             context[piece, rows, :] = summed[:, piece * 128 : (piece + 1) * 128]
 
-    load_queries.wait()
     value_ring.relay(1)
     swap.wait_recv()
     chunks = list(range(0, tokens * heads, ROWS))
@@ -439,6 +428,9 @@
             attend(start)
         done = until
         value_ring.relay(step)
+        if step == 2:
+            for copy in spreads:
+                copy.start()
     for h in range(heads):
         rows = jnp.concatenate(
             [context[piece, pl.ds(h, tokens, stride=heads), :] for piece in range(latent // 128)], axis=1
@@ -454,10 +446,6 @@
         heads_send, heads_recv,
     )
     heads_ring.launch()
-    load_proj.wait()
-    for copy in spreads:
-        copy.wait_recv()
-    load_router.wait()
     pieces = Pieces(count, held, piece_send, piece_recv, side_send, side_recv)
     pairs = {}
 
@@ -470,13 +458,16 @@
         mine[number, 0] = product[:, :part]
         mine[number, 1] = product[:, part:]
         copy = remote(
-            mine.at[number, 1 - core], theirs.at[number], pair_send.at[number], pair_recv.at[number],
+            mine.at[number, 1 - core], theirs.at[number], pair_send, pair_recv.at[number],
             {"tp": 1 - core},
         )
         copy.start()
         pairs[number] = copy
 
     def conclude(number):
+        if number == 0:
+            drain(residual.at[: count - 1], res_sem.at[1])
+            drain(ids_all.at[: count - 1], id_sem.at[1])
         pairs[number].wait_recv()
         block = block_at(offset_of(number, count))
         attention = mine[number, core] + theirs[number]
@@ -516,9 +507,8 @@
         share_here = local_v[1, first, :].astype(bf16).astype(f32)
         rank = jnp.dot(here.astype(bf16), before, preferred_element_type=f32)
         hits = (here[:, None, :] > 0.5) & (rank[:, None, :] == slot)
-        mixing[index] = (
-            jnp.where(hits, share_here[:, None, :], 0.0).reshape(local * CAP, tokens).astype(bf16)
-        )
+        mixed = jnp.where(hits, share_here[:, None, :], 0.0).reshape(local * CAP, tokens)
+        mixing[index] = mixed.T.astype(bf16)
         chosen = jnp.dot(
             jnp.where(hits, 1.0, 0.0).reshape(local * CAP, tokens).astype(bf16), normed,
             preferred_element_type=f32,
@@ -548,16 +538,10 @@
         [held[me, (count // 2) * core + e, c] for e in range(count // 2) for c in range(2)], axis=1
     )
 
-    def weights(number, expert):
-        span = pl.ds(expert * blocks, blocks)
-        source, target = ((gate_hbm, gate), (up_hbm, up), (down_hbm, down))[number]
-        return pltpu.make_async_copy(source.at[span], target.at[span], weight_sem.at[number, expert])
-
     inner = blocks * gate.shape[1]
 
     def excite(expert, carry):
-        weights(0, expert).wait()
-        weights(1, expert).wait()
+        drain(gate.at[: 2 * blocks], excite_sem.at[expert])
         span = pl.ds(expert * blocks, blocks)
         slots = picked[expert].astype(bf16)
         dims = (((1,), (1,)), ((), ()))
@@ -568,8 +552,7 @@
         return carry
 
     lax.fori_loop(0, local, excite, 0)
-    for expert in range(local):
-        weights(2, expert).wait()
+    load_down.wait()
 
     piece = sums.shape[4]
     turns = sums.shape[0]
@@ -579,32 +562,31 @@
     steps = list(range(1, pair)) + [0]
     near_order = [lax.rem(me + 2 * step, count) for step in steps]
     twin_order = [lax.rem(twin + 2 * step, count) for step in steps]
-    boths, crosses, backs = {}, {}, {}
+    boths, crosses = {}, {}
 
     def lower(turn):
-        def one(expert, carry):
+        rows = []
+        for expert in range(local):
             span = pl.ds(expert * blocks, blocks)
-            for c in range(2):
-                column = pl.ds(c * side_width + turn * piece, piece)
-                rows_v[expert, :, c * piece : (c + 1) * piece] = jnp.dot(
-                    active[expert], down[span, :, column].reshape(inner, piece),
+            sides = [
+                jnp.dot(
+                    active[expert],
+                    down[span, :, pl.ds(c * side_width + turn * piece, piece)].reshape(inner, piece),
                     preferred_element_type=f32,
                 )
-            return carry
-
-        lax.fori_loop(0, local, one, 0)
+                for c in range(2)
+            ]
+            rows.append(jnp.concatenate(sides, axis=1))
         for offset in range(count):
-            rows = jnp.concatenate(
-                [rows_v[e, offset * CAP : (offset + 1) * CAP, :] for e in range(local)], axis=0
-            ).astype(bf16)
-            mixed = lax.dot_general(
-                mixing[offset], rows, (((0,), (0,)), ((), ())), preferred_element_type=f32
+            mine_rows = [row[offset * CAP : (offset + 1) * CAP] for row in rows]
+            mixed = jnp.dot(
+                mixing[offset], jnp.concatenate(mine_rows, axis=0).astype(bf16), preferred_element_type=f32
             ).astype(bf16)
             block = block_at(offset)
             for c in range(2):
                 sums[turn, c, block] = mixed[:, c * piece : (c + 1) * piece]
         boths[turn] = remote(
-            sums.at[turn, 1 - core], sums2.at[turn], both_send.at[turn], both_recv.at[turn],
+            sums.at[turn, 1 - core], sums2.at[turn], both_send, both_recv.at[turn],
             {"tp": 1 - core},
         )
         boths[turn].start()
@@ -617,7 +599,7 @@
         for i, block in enumerate(twin_order):
             outbox[turn, i] = added(turn, block).astype(bf16)
         crosses[turn] = remote(
-            outbox.at[turn], inbox.at[turn], cross_send.at[turn], cross_recv.at[turn], {"ep": twin}
+            outbox.at[turn], inbox.at[turn], cross_send, cross_recv.at[turn], {"ep": twin}
         )
         crosses[turn].start()
 
@@ -629,45 +611,44 @@
                 totals[turn] = total
                 continue
             outbox2[turn, i] = total.astype(bf16)
-            backs[turn, i] = remote(
-                outbox2.at[turn, i], inbox2.at[turn, i], back_send.at[turn, i], back_recv.at[turn, i],
-                {"ep": block},
-            )
-            backs[turn, i].start()
+            remote(
+                outbox2.at[turn, i], inbox2.at[turn, i], back_send, back_recv.at[turn], {"ep": block}
+            ).start()
 
     def end(turn):
         total = totals[turn]
+        drain(inbox2.at[turn], back_recv.at[turn])
         for i in range(pair - 1):
-            backs[turn, i].wait_recv()
             total = total + inbox2[turn, i].astype(f32)
         out_ref[:, turn * piece : (turn + 1) * piece] = total.astype(bf16)
 
-    for turn in range(turns):
-        lower(turn)
-        if turn >= 1:
+    for turn in range(turns + 3):
+        if turn < turns:
+            lower(turn)
+        if 1 <= turn <= turns:
             cross(turn - 1)
-    cross(turns - 1)
-    for turn in range(turns):
-        back(turn)
+        if turn >= 3:
+            back(turn - 3)
     for turn in range(turns):
         end(turn)
 
-    value_ring.finish()
-    heads_ring.finish()
+    drain(values.at[:, : count - 1], value_send)
+    drain(heads_all.at[: count - 1], heads_send)
     pieces.finish()
     swap.wait_send()
-    for copy in spreads:
-        copy.wait_send()
-    for group in (pairs, boths, crosses, backs):
-        for copy in group.values():
-            copy.wait_send()
+    drain(residual.at[: count - 1], res_sem.at[0])
+    drain(ids_all.at[: count - 1], id_sem.at[0])
+    drain(theirs, pair_send)
+    drain(sums2, both_send)
+    drain(inbox, cross_send)
+    drain(inbox2, back_send)
 
 
 def dma(*shape):
     return pltpu.SemaphoreType.DMA(shape)
 
 
-TURNS = 4
+TURNS = 8
 
 
 def lean_body(
@@ -698,8 +679,6 @@
     blocks = gate_weight.shape[0] // local
     hidden_here = gate_weight.shape[2]
     piece = model // 2 // TURNS
-    meta = jnp.concatenate([expert_ids.T, token_visible[None], token_request[None]], axis=0)
-    meta = jnp.pad(meta, ((0, 8 - meta.shape[0]), (0, 128 - tokens)))
     whole = pl.BlockSpec(memory_space=pltpu.VMEM)
     anywhere = pl.BlockSpec(memory_space=pl.ANY)
     vmem = pltpu.VMEM
@@ -707,7 +686,7 @@
     hidden, expert_out = pl.pallas_call(
         functools.partial(layer_kernel, count),
         out_shape=(shape((tokens, model // 2), bf16), shape((tokens, model // 2), bf16)),
-        in_specs=[whole] * 2 + [anywhere] * 9,
+        in_specs=[whole] * 4 + [anywhere] * 9,
         out_specs=(whole, whole),
         scratch_shapes=[
             vmem((tokens * heads, columns), bf16),
@@ -730,9 +709,8 @@
             vmem((count, 8, 128), jnp.int32),
             vmem((2, EXPERTS, tokens), f32),
             vmem((local, slots, model), f32),
-            vmem((count, local * CAP, tokens), bf16),
+            vmem((count, tokens, local * CAP), bf16),
             vmem((local, slots, blocks * hidden_here), bf16),
-            vmem((local, slots, 2 * piece), f32),
             vmem((TURNS, 2, count, tokens, piece), bf16),
             vmem((TURNS, count, tokens, piece), bf16),
             vmem((TURNS, far, tokens, piece), bf16),
@@ -740,16 +718,16 @@
             vmem((TURNS, far - 1, tokens, piece), bf16),
             vmem((TURNS, far - 1, tokens, piece), bf16),
             vmem((TURNS, tokens, piece), f32),
-            dma(6), dma(3, local), dma(2), dma(count - 1), dma(count - 1), dma(count - 1), dma(count - 1),
-            dma(2, far, 2), dma(2, far, 2), dma(2, far, 2), dma(2, far, 2), dma(count), dma(count),
-            dma(count, 2, far), dma(count, 2, far), dma(count, count), dma(count, count),
-            dma(TURNS), dma(TURNS), dma(TURNS), dma(TURNS), dma(TURNS, far - 1), dma(TURNS, far - 1),
+            dma(6), dma(local), dma(), dma(2), dma(2), dma(2),
+            dma(), dma(2, far, PARTS), dma(), dma(2, far, PARTS), dma(), dma(count),
+            dma(), dma(count, 2, far), dma(), dma(count),
+            dma(), dma(TURNS), dma(), dma(TURNS), dma(), dma(TURNS),
         ],
         compiler_params=pltpu.CompilerParams(
-            collective_id=0, has_side_effects=True, vmem_limit_bytes=63 * 2**20
+            collective_id=0, has_side_effects=True, vmem_limit_bytes=59 * 2**20
         ),
     )(
-        meta, norm_gain.reshape(1, model), queries.reshape(tokens * heads, columns),
+        expert_ids.T, token_visible[None], token_request[None], norm_gain[None], queries.reshape(tokens * heads, columns),
         jnp.swapaxes(latent_cache, 1, 2), value_proj, out_proj, residual, router.T,
         jnp.swapaxes(gate_weight, 1, 2), jnp.swapaxes(up_weight, 1, 2), down_weight,
     )

time: 101 us -> 86.9 us (0.86)
  Pallas kernels: 96.1 us -> 82.9 us
    pallas_call x1, Pallas kernels: 96.1 us -> 82.9 us  [lean_body(): pl.pallas_call(functools.partial(layer_kernel, count), out_shape=(shape((...]
where the time goes in v2:
time: 86.9 us; the launch traced here: 86.7 us
  Pallas kernels  82.9 us (95%)
  local copies, waits for them, and re-layouts  3.14 us (4%)
    pallas_call x1, Pallas kernels, lean_body(): pl.pallas_call(functools.partial(layer_kernel, count), out_shape=(shape((...  82.9 us
    unnamed x2, local copies, waits for them, and re-layouts  3.14 us

profile of v2, /device:TPU:0, one launch (start us, length us, event | category | flops | bytes accessed | tf_op | source)
XLA Modules:
  0.0 86.7 jit_solution(17819853096187556226)
XLA Ops:
  0.6 82.9 %shard_map.140 = (bf16[64,1024]{1,0:T(8,128)(2,1)}, bf16[64,1024]{1,0:T(8,128)(2,1)}) custom-call(s32[6,64]{1,0:T(8,128)} %bitcast.15, s32[1,64]{1,0:T(1,128)} %bitcast.16, s32[1,64]{1,0:T(1,128)} %bitcast.17, f32[1,2048]{1,0:T(1,128)} %bitcast.14, bf16[512,576]{1,0:T(8,128)(2,1)} %bitcast.12, bf16[3,576,256]{2,1,0:T(8,128)(2,1)} %bitcast.11, ...), custom_call_target="tpu_custom_call" | custom-call | tf_op jit(solution)/shard_map/pallas_call | solution.py:686
  83.5 1.6 %copy.17 = bf16[64,1024]{1,0:T(8,128)(2,1)} copy(bf16[64,1024]{1,0:T(8,128)(2,1)} %get-tuple-element.4) | data formatting | bytes 262144
  85.1 1.6 %copy.18 = bf16[64,1024]{1,0:T(8,128)(2,1)} copy(bf16[64,1024]{1,0:T(8,128)(2,1)} %get-tuple-element.5) | data formatting | bytes 262144

commit v3 on v2

--- a/solution.py
+++ b/solution.py
@@ -280,8 +280,7 @@
 
     def side(self, offset, number):
         ref = self.piece(offset, number)
-        where = (offset + offset_of(number, self.count)) % self.count
-        remote(ref, ref, self.sems[2], self.sems[3].at[where], {"tp": 1 - self.core}).start()
+        remote(ref, ref, self.sems[2], self.sems[3].at[offset % self.count], {"tp": 1 - self.core}).start()
 
     def launch(self, number):
         for turn in range(2):
@@ -321,7 +320,7 @@
     count, ids_ref, visible_ref, request_ref, gain_ref, queries_hbm, cache_hbm, value_hbm, proj_hbm, residual_hbm, router_hbm,
     gate_hbm, up_hbm, down_hbm, hidden_ref, out_ref,
     queries, cache, values, proj, residual_own, residual, router, gate, up, down,
-    limits, context, heads_own, heads_all, mine, theirs, held, ids_all, local_v, picked, mixing, active,
+    limits, context, heads_own, heads_all, mine, theirs, held, ids_all, ids_row, hits, squares, logits_v, excited, mixing, active,
     sums, sums2, outbox, inbox, outbox2, inbox2, totals,
     load_sem, excite_sem, lower_sem, swap_sem, id_sem, res_sem,
     value_send, value_recv, heads_send, heads_recv, pair_send, pair_recv,
@@ -474,48 +473,99 @@
         held[block, me, core] = (residual[block].astype(f32) + attention).astype(bf16)
         pieces.launch(number)
 
-    expert_row = lax.broadcasted_iota(jnp.int32, (EXPERTS, tokens), 0)
-    before = (
-        lax.broadcasted_iota(jnp.int32, (tokens, tokens), 0)
-        < lax.broadcasted_iota(jnp.int32, (tokens, tokens), 1)
-    ).astype(bf16)
-    slot = lax.broadcasted_iota(jnp.int32, (local, CAP, tokens), 1).astype(f32)
-
-    def route(offset):
+    around = [offset if offset <= far else offset - count for offset in range(count)]
+    dims = (((1,), (1,)), ((), ()))
+    inner = blocks * gate.shape[1]
+
+    def place_slots():
+        before = (
+            lax.broadcasted_iota(jnp.int32, (tokens, tokens), 0)
+            < lax.broadcasted_iota(jnp.int32, (tokens, tokens), 1)
+        ).astype(bf16)
+        ids = [ids_all[block_at(offset)][:, :tokens] for offset in around]
+        ids_row[...] = jnp.concatenate(ids, axis=1)
+        expert = lax.broadcasted_iota(jnp.int32, (local, tokens), 0) + me * local
+        here = []
+        for one in ids:
+            named = expert == one[0:1]
+            for k in range(1, TOPK):
+                named = named | (expert == one[k : k + 1])
+            here.append(named.astype(f32))
+        here = jnp.concatenate(here, axis=0)
+        rank = jnp.dot(here.astype(bf16), before, preferred_element_type=f32)
+        slot = lax.broadcasted_iota(jnp.int32, (count * local, CAP, tokens), 1).astype(f32)
+        hit = (here[:, None, :] > 0.5) & (rank[:, None, :] == slot)
+        hits[...] = jnp.where(hit, 1.0, 0.0).reshape(count, local * CAP, tokens).astype(bf16)
+
+    def contract(offset):
         pieces.settle(offset)
-        block = block_at(offset)
-        index = offset % count
-        wide = jnp.concatenate(
-            [held[block, e, c] for e in range(count) for c in range(2)], axis=1
-        ).astype(f32)
-        scale = lax.rsqrt(jnp.mean(wide * wide, axis=1, keepdims=True) + epsilon)
-        normed = (wide * scale * gain_ref[...]).astype(bf16)
-        logits = lax.dot_general(
-            router[...], normed, (((1,), (1,)), ((), ())), preferred_element_type=f32
+        owner = block_at(offset)
+        column = pl.ds(pl.multiple_of(owner * width, width), width)
+        gain = gain_ref[pl.ds(owner, 1), :]
+        first = offset == 0
+        scaled, chosen = [], []
+        for index, other in enumerate(around):
+            span = pl.ds(index * tokens, tokens)
+            block = block_at(other)
+            sides = [held[block, owner, c].astype(f32) for c in range(2)]
+            square = sides[0] * sides[0] + sides[1] * sides[1]
+            squares[span, :] = square if first else squares[span, :] + square
+            wide = (jnp.concatenate(sides, axis=1) * gain).astype(bf16)
+            scaled.append(wide)
+            chosen.append(jnp.dot(hits[index], wide, preferred_element_type=f32))
+        part_logits = lax.dot_general(
+            router[:, column], jnp.concatenate(scaled, axis=0), dims, preferred_element_type=f32
         )
-        ids = ids_all[block][:TOPK, :tokens]
-        named = expert_row == ids[0:1]
+        logits_v[...] = part_logits if first else logits_v[...] + part_logits
+        for expert in range(local):
+            if first:
+                drain(gate.at[: 2 * blocks], excite_sem.at[expert])
+            slots = jnp.concatenate(
+                [one[expert * CAP : (expert + 1) * CAP] for one in chosen], axis=0
+            ).astype(bf16)
+            span = pl.ds(expert * blocks, blocks)
+            for number, weight in enumerate((gate, up)):
+                term = lax.dot_general(
+                    weight[span, :, column].reshape(inner, width), slots, dims, preferred_element_type=f32
+                )
+                rows = pl.ds(number * inner, inner)
+                excited[expert, rows, :] = term if first else excited[expert, rows, :] + term
+
+    def activate():
+        mean = jnp.sum(squares[...], axis=1, keepdims=True) / model
+        scale = jnp.broadcast_to(lax.rsqrt(mean + epsilon), squares.shape).T[:1]
+        lane = lax.broadcasted_iota(jnp.int32, (count * CAP, 128), 1)
+        slot_scale = jnp.zeros((count * CAP, 128), f32)
+        slot_scales = [
+            jnp.sum(hits[index].astype(f32) * scale[:, index * tokens : (index + 1) * tokens], axis=1, keepdims=True)
+            for index in range(count)
+        ]
+        for expert in range(local):
+            own = jnp.concatenate([one[expert * CAP : (expert + 1) * CAP] for one in slot_scales], axis=0)
+            slot_scale = jnp.where(lane == expert, own, slot_scale)
+        slot_scale = slot_scale.T
+        for expert in range(local):
+            row = slot_scale[expert : expert + 1]
+            gate_t = excited[expert, :inner, :] * row
+            up_t = excited[expert, inner:, :] * row
+            active[expert] = (gate_t / (1.0 + jnp.exp(-gate_t)) * up_t).T.astype(bf16)
+        expert_row = lax.broadcasted_iota(jnp.int32, (EXPERTS, count * tokens), 0)
+        named = expert_row == ids_row[0:1, :]
         for k in range(1, TOPK):
-            named = named | (expert_row == ids[k : k + 1])
-        logits = jnp.where(named, logits, -jnp.inf)
+            named = named | (expert_row == ids_row[k : k + 1, :])
+        logits = jnp.where(named, logits_v[...] * scale, -jnp.inf)
         raised = jnp.exp(logits - jnp.max(logits, axis=0, keepdims=True))
-        share = raised / jnp.sum(raised, axis=0, keepdims=True)
-        local_v[0] = named.astype(f32)
-        local_v[1] = share
-        first = pl.ds(pl.multiple_of(me * local, local), local)
-        here = local_v[0, first, :]
-        share_here = local_v[1, first, :].astype(bf16).astype(f32)
-        rank = jnp.dot(here.astype(bf16), before, preferred_element_type=f32)
-        hits = (here[:, None, :] > 0.5) & (rank[:, None, :] == slot)
-        mixed = jnp.where(hits, share_here[:, None, :], 0.0).reshape(local * CAP, tokens)
-        mixing[index] = mixed.T.astype(bf16)
-        chosen = jnp.dot(
-            jnp.where(hits, 1.0, 0.0).reshape(local * CAP, tokens).astype(bf16), normed,
-            preferred_element_type=f32,
-        )
-        for e in range(local):
-            picked[e, pl.ds(index * CAP, CAP), :] = chosen[e * CAP : (e + 1) * CAP]
-
+        logits_v[...] = raised / jnp.sum(raised, axis=0, keepdims=True)
+        share = logits_v[pl.ds(pl.multiple_of(me * local, local), local), :].astype(bf16).astype(f32)
+        for index in range(count):
+            own = share[:, None, index * tokens : (index + 1) * tokens]
+            own = jnp.broadcast_to(own, (local, CAP, tokens)).reshape(local * CAP, tokens)
+            mixing[index] = (hits[index].astype(f32) * own).T.astype(bf16)
+
+    due = {far: [0], far + 1: [1]}
+    for distance in range(2, far):
+        due[far + distance] = [1 - distance, distance]
+    due[2 * far] = [1 - far, far]
     for turn in range(2 * far + 1):
         if 1 <= turn <= far:
             heads_ring.relay(turn)
@@ -529,29 +579,16 @@
         if turn <= far:
             for number in group_of(turn, count):
                 conclude(number)
-        if turn >= far:
-            for offset in sorted({2 * far - turn, turn - 2 * far}):
-                if offset != -far:
-                    route(offset)
+        if turn == 0:
+            place_slots()
+        for offset in due.get(turn, ()):
+            contract(offset)
+    activate()
 
     hidden_ref[...] = jnp.concatenate(
         [held[me, (count // 2) * core + e, c] for e in range(count // 2) for c in range(2)], axis=1
     )
 
-    inner = blocks * gate.shape[1]
-
-    def excite(expert, carry):
-        drain(gate.at[: 2 * blocks], excite_sem.at[expert])
-        span = pl.ds(expert * blocks, blocks)
-        slots = picked[expert].astype(bf16)
-        dims = (((1,), (1,)), ((), ()))
-        gate_t = lax.dot_general(gate[span].reshape(inner, model), slots, dims, preferred_element_type=f32)
-        up_t = lax.dot_general(up[span].reshape(inner, model), slots, dims, preferred_element_type=f32)
-        active_t = gate_t / (1.0 + jnp.exp(-gate_t)) * up_t
-        active[expert] = active_t.T.astype(bf16)
-        return carry
-
-    lax.fori_loop(0, local, excite, 0)
     load_down.wait()
 
     piece = sums.shape[4]
@@ -707,8 +744,11 @@
             vmem((count, tokens, width // 2), f32),
             vmem((count, count, 2, tokens, width // 2), bf16),
             vmem((count, 8, 128), jnp.int32),
-            vmem((2, EXPERTS, tokens), f32),
-            vmem((local, slots, model), f32),
+            vmem((8, count * tokens), jnp.int32),
+            vmem((count, local * CAP, tokens), bf16),
+            vmem((count * tokens, 128), f32),
+            vmem((EXPERTS, count * tokens), f32),
+            vmem((local, 2 * blocks * hidden_here, slots), f32),
             vmem((count, tokens, local * CAP), bf16),
             vmem((local, slots, blocks * hidden_here), bf16),
             vmem((TURNS, 2, count, tokens, piece), bf16),
@@ -727,7 +767,7 @@
             collective_id=0, has_side_effects=True, vmem_limit_bytes=59 * 2**20
         ),
     )(
-        expert_ids.T, token_visible[None], token_request[None], norm_gain[None], queries.reshape(tokens * heads, columns),
+        expert_ids.T, token_visible[None], token_request[None], norm_gain.reshape(count, model // count), queries.reshape(tokens * heads, columns),
         jnp.swapaxes(latent_cache, 1, 2), value_proj, out_proj, residual, router.T,
         jnp.swapaxes(gate_weight, 1, 2), jnp.swapaxes(up_weight, 1, 2), down_weight,
     )

time: 86.9 us -> 82.1 us (0.945)
  Pallas kernels: 82.9 us -> 76.7 us
  local copies, waits for them, and re-layouts: 3.14 us -> 4.43 us
    pallas_call x1, Pallas kernels: 82.9 us -> 76.7 us  [lean_body(): pl.pallas_call(functools.partial(layer_kernel, count), out_shape=(shape((...]
    reshape x0 -> x1, local copies, waits for them, and re-layouts: none -> 1.3 us  [lean_body(): norm_gain.reshape(count, model // count)]
where the time goes in v3:
time: 82.1 us; the launch traced here: 81.8 us
  Pallas kernels  76.7 us (93%)
  local copies, waits for them, and re-layouts  4.43 us (5%)
    pallas_call x1, Pallas kernels, lean_body(): pl.pallas_call(functools.partial(layer_kernel, count), out_shape=(shape((...  76.7 us
    unnamed x2, local copies, waits for them, and re-layouts  3.14 us

profile of v3, /device:TPU:0, one launch (start us, length us, event | category | flops | bytes accessed | tf_op | source)
XLA Modules:
  0.0 81.8 jit_solution(7096831767945909618)
XLA Ops:
  0.6 1.3 %reshape.10.gain_ref = f32[8,256]{1,0:T(8,128)} reshape(f32[2048]{0:T(1024)} %param.20) | data formatting | bytes 16384 | tf_op jit(solution)/shard_map/reshape | solution.py:770
  1.9 76.7 %shard_map.140 = (bf16[64,1024]{1,0:T(8,128)(2,1)}, bf16[64,1024]{1,0:T(8,128)(2,1)}) custom-call(s32[6,64]{1,0:T(8,128)} %bitcast.13, s32[1,64]{1,0:T(1,128)} %bitcast.14, s32[1,64]{1,0:T(1,128)} %bitcast.15, f32[8,256]{1,0:T(8,128)} %reshape.10.gain_ref, bf16[512,576]{1,0:T(8,128)(2,1)} %bitcast.11, bf16[3,576,256]{2,1,0:T(8,128)(2,1)} %bitcast.10, ...), custom_call_target="tpu_custom_call" | custom-call | tf_op jit(solution)/shard_map/pallas_call | solution.py:723
  78.7 1.6 %copy.17 = bf16[64,1024]{1,0:T(8,128)(2,1)} copy(bf16[64,1024]{1,0:T(8,128)(2,1)} %get-tuple-element.4) | data formatting | bytes 262144
  80.2 1.6 %copy.18 = bf16[64,1024]{1,0:T(8,128)(2,1)} copy(bf16[64,1024]{1,0:T(8,128)(2,1)} %get-tuple-element.5) | data formatting | bytes 262144

commit v4 on v3

--- a/solution.py
+++ b/solution.py
@@ -317,15 +317,16 @@
 
 
 def layer_kernel(
-    count, ids_ref, visible_ref, request_ref, gain_ref, queries_hbm, cache_hbm, value_hbm, proj_hbm, residual_hbm, router_hbm,
-    gate_hbm, up_hbm, down_hbm, hidden_ref, out_ref,
+    count, ids_hbm, visible_hbm, request_hbm, gain_hbm, queries_hbm, cache_hbm, value_hbm, proj_hbm, residual_hbm, router_hbm,
+    gate_hbm, up_hbm, down_hbm, hidden_hbm, out_hbm,
+    ids_ref, visible_ref, request_ref, gain_ref,
     queries, cache, values, proj, residual_own, residual, router, gate, up, down,
-    limits, context, heads_own, heads_all, mine, theirs, held, ids_all, ids_row, hits, squares, logits_v, excited, mixing, active,
-    sums, sums2, outbox, inbox, outbox2, inbox2, totals,
+    limits, context, heads_own, heads_all, theirs, held, ids_all, ids_row, hits, logits_v, scales, excited, mixing, active,
+    sums2, inbox, inbox2,
     load_sem, excite_sem, lower_sem, swap_sem, id_sem, res_sem,
     value_send, value_recv, heads_send, heads_recv, pair_send, pair_recv,
     piece_send, piece_recv, side_send, side_recv,
-    both_send, both_recv, cross_send, cross_recv, back_send, back_recv,
+    both_send, both_recv, cross_send, cross_recv, back_send, back_recv, store_sem,
 ):
     me = lax.axis_index("ep")
     core = lax.axis_index("tp")
@@ -345,11 +346,16 @@
 
     load_value = copy_here(value_hbm, values.at[:, me], load_sem.at[0])
     load_cache = copy_here(cache_hbm, cache.at[core], load_sem.at[1])
+    load_small = [
+        copy_here(source, target, load_sem.at[6 + number])
+        for number, (source, target) in enumerate(
+            ((ids_hbm, ids_ref), (visible_hbm, visible_ref), (request_hbm, request_ref), (gain_hbm, gain_ref))
+        )
+    ]
     load_residual = copy_here(residual_hbm, residual_own, load_sem.at[2])
     load_queries = copy_here(queries_hbm, queries, load_sem.at[3])
     load_proj = copy_here(proj_hbm, proj, load_sem.at[4])
     load_router = copy_here(router_hbm, router, load_sem.at[5])
-    ids_all[me, :TOPK, :tokens] = ids_ref[...]
     greet(count)
 
     load_value.wait()
@@ -360,6 +366,9 @@
         value_send, value_recv,
     )
     value_ring.launch()
+    for copy in load_small:
+        copy.wait()
+    ids_all[me, :TOPK, :tokens] = ids_ref[...]
     load_cache.wait()
     swap = remote(cache.at[core], cache.at[core], swap_sem.at[0], swap_sem.at[1], {"tp": 1 - core})
     swap.start()
@@ -370,7 +379,7 @@
     for expert in range(local):
         span = pl.ds(expert * blocks, blocks)
         for source, target in ((gate_hbm, gate), (up_hbm, up)):
-            pltpu.make_async_copy(source.at[span], target.at[span], excite_sem.at[expert]).start()
+            pltpu.make_async_copy(source.at[span], target.at[span], excite_sem).start()
     load_down = copy_here(down_hbm, down, lower_sem)
     spreads = []
     for step in range(1, count):
@@ -445,6 +454,7 @@
         heads_send, heads_recv,
     )
     heads_ring.launch()
+    mine = context
     pieces = Pieces(count, held, piece_send, piece_recv, side_send, side_recv)
     pairs = {}
 
@@ -454,10 +464,11 @@
     def project(number):
         rows = heads_own[...] if number == 0 else heads_all[block_at(offset_of(number, count))]
         product = jnp.dot(rows, proj[...], preferred_element_type=f32)
-        mine[number, 0] = product[:, :part]
-        mine[number, 1] = product[:, part:]
+        rows = pl.ds(number * tokens, tokens)
+        mine[0, rows, :] = product[:, :part]
+        mine[1, rows, :] = product[:, part:]
         copy = remote(
-            mine.at[number, 1 - core], theirs.at[number], pair_send, pair_recv.at[number],
+            mine.at[1 - core, rows, :], theirs.at[number], pair_send, pair_recv.at[number],
             {"tp": 1 - core},
         )
         copy.start()
@@ -469,10 +480,11 @@
             drain(ids_all.at[: count - 1], id_sem.at[1])
         pairs[number].wait_recv()
         block = block_at(offset_of(number, count))
-        attention = mine[number, core] + theirs[number]
+        attention = mine[core, pl.ds(number * tokens, tokens), :] + theirs[number]
         held[block, me, core] = (residual[block].astype(f32) + attention).astype(bf16)
         pieces.launch(number)
 
+    squares = limits
     around = [offset if offset <= far else offset - count for offset in range(count)]
     dims = (((1,), (1,)), ((), ()))
     inner = blocks * gate.shape[1]
@@ -497,11 +509,12 @@
         hit = (here[:, None, :] > 0.5) & (rank[:, None, :] == slot)
         hits[...] = jnp.where(hit, 1.0, 0.0).reshape(count, local * CAP, tokens).astype(bf16)
 
-    def contract(offset):
-        pieces.settle(offset)
+    def columns_of(offset):
+        return pl.ds(pl.multiple_of(block_at(offset) * width, width), width)
+
+    def prepare(offset):
         owner = block_at(offset)
-        column = pl.ds(pl.multiple_of(owner * width, width), width)
-        gain = gain_ref[pl.ds(owner, 1), :]
+        gain = gain_ref[:, columns_of(offset)]
         first = offset == 0
         scaled, chosen = [], []
         for index, other in enumerate(around):
@@ -514,24 +527,34 @@
             scaled.append(wide)
             chosen.append(jnp.dot(hits[index], wide, preferred_element_type=f32))
         part_logits = lax.dot_general(
-            router[:, column], jnp.concatenate(scaled, axis=0), dims, preferred_element_type=f32
+            router[:, columns_of(offset)], jnp.concatenate(scaled, axis=0), dims, preferred_element_type=f32
         )
         logits_v[...] = part_logits if first else logits_v[...] + part_logits
-        for expert in range(local):
-            if first:
-                drain(gate.at[: 2 * blocks], excite_sem.at[expert])
-            slots = jnp.concatenate(
+        return [
+            jnp.concatenate(
                 [one[expert * CAP : (expert + 1) * CAP] for one in chosen], axis=0
             ).astype(bf16)
+            for expert in range(local)
+        ]
+
+    def stream(offset, slots):
+        column = columns_of(offset)
+        for expert in range(local):
             span = pl.ds(expert * blocks, blocks)
-            for number, weight in enumerate((gate, up)):
-                term = lax.dot_general(
-                    weight[span, :, column].reshape(inner, width), slots, dims, preferred_element_type=f32
-                )
-                rows = pl.ds(number * inner, inner)
-                excited[expert, rows, :] = term if first else excited[expert, rows, :] + term
-
-    def activate():
+            weights = jnp.concatenate(
+                [weight[span, :, column].reshape(inner, width) for weight in (gate, up)], axis=0
+            )
+            term = lax.dot_general(weights, slots[expert], dims, preferred_element_type=f32)
+            excited[expert] = term if offset == 0 else excited[expert] + term
+
+    def contract(offset, last=False):
+        pieces.settle(offset)
+        slots = prepare(offset)
+        if last:
+            weigh()
+        stream(offset, slots)
+
+    def weigh():
         mean = jnp.sum(squares[...], axis=1, keepdims=True) / model
         scale = jnp.broadcast_to(lax.rsqrt(mean + epsilon), squares.shape).T[:1]
         lane = lax.broadcasted_iota(jnp.int32, (count * CAP, 128), 1)
@@ -543,12 +566,7 @@
         for expert in range(local):
             own = jnp.concatenate([one[expert * CAP : (expert + 1) * CAP] for one in slot_scales], axis=0)
             slot_scale = jnp.where(lane == expert, own, slot_scale)
-        slot_scale = slot_scale.T
-        for expert in range(local):
-            row = slot_scale[expert : expert + 1]
-            gate_t = excited[expert, :inner, :] * row
-            up_t = excited[expert, inner:, :] * row
-            active[expert] = (gate_t / (1.0 + jnp.exp(-gate_t)) * up_t).T.astype(bf16)
+        scales[...] = slot_scale.T[:local]
         expert_row = lax.broadcasted_iota(jnp.int32, (EXPERTS, count * tokens), 0)
         named = expert_row == ids_row[0:1, :]
         for k in range(1, TOPK):
@@ -562,11 +580,21 @@
             own = jnp.broadcast_to(own, (local, CAP, tokens)).reshape(local * CAP, tokens)
             mixing[index] = (hits[index].astype(f32) * own).T.astype(bf16)
 
+    def activate():
+        for expert in range(local):
+            row = scales[expert : expert + 1]
+            gate_t = excited[expert, :inner, :] * row
+            up_t = excited[expert, inner:, :] * row
+            active[expert] = (gate_t / (1.0 + jnp.exp(-gate_t)) * up_t).T.astype(bf16)
+
     due = {far: [0], far + 1: [1]}
     for distance in range(2, far):
         due[far + distance] = [1 - distance, distance]
     due[2 * far] = [1 - far, far]
     for turn in range(2 * far + 1):
+        if turn == far:
+            drain(gate, excite_sem)
+            drain(up, excite_sem)
         if 1 <= turn <= far:
             heads_ring.relay(turn)
         if turn <= far:
@@ -582,17 +610,22 @@
         if turn == 0:
             place_slots()
         for offset in due.get(turn, ()):
-            contract(offset)
+            contract(offset, offset == far)
     activate()
 
-    hidden_ref[...] = jnp.concatenate(
-        [held[me, (count // 2) * core + e, c] for e in range(count // 2) for c in range(2)], axis=1
-    )
-
+    for e in range(count // 2):
+        for c in range(2):
+            number = 2 * e + c
+            copy_here(
+                held.at[me, (count // 2) * core + e, c],
+                hidden_hbm.at[:, pl.ds(number * part, part)],
+                store_sem.at[0],
+            )
     load_down.wait()
 
-    piece = sums.shape[4]
-    turns = sums.shape[0]
+    turns = sums2.shape[0]
+    piece = sums2.shape[2] // count
+    sums = gate
     side_width = model // 2
     twin = me + 1 - 2 * lax.rem(me, 2)
     pair = count // 2
@@ -600,6 +633,9 @@
     near_order = [lax.rem(me + 2 * step, count) for step in steps]
     twin_order = [lax.rem(twin + 2 * step, count) for step in steps]
     boths, crosses = {}, {}
+
+    def lanes_of(block):
+        return pl.ds(pl.multiple_of(block * piece, piece), piece)
 
     def lower(turn):
         rows = []
@@ -619,45 +655,55 @@
             mixed = jnp.dot(
                 mixing[offset], jnp.concatenate(mine_rows, axis=0).astype(bf16), preferred_element_type=f32
             ).astype(bf16)
-            block = block_at(offset)
             for c in range(2):
-                sums[turn, c, block] = mixed[:, c * piece : (c + 1) * piece]
+                sums[2 * turn + c, :tokens, lanes_of(block_at(offset))] = mixed[:, c * piece : (c + 1) * piece]
         boths[turn] = remote(
-            sums.at[turn, 1 - core], sums2.at[turn], both_send, both_recv.at[turn],
+            sums.at[2 * turn + 1 - core, pl.ds(0, tokens), pl.ds(0, count * piece)], sums2.at[turn], both_send, both_recv.at[turn],
             {"tp": 1 - core},
         )
         boths[turn].start()
 
     def added(turn, block):
-        return sums[turn, core, block].astype(f32) + sums2[turn, block].astype(f32)
+        own = sums[2 * turn + core, :tokens, lanes_of(block)]
+        return own.astype(f32) + sums2[turn, :, lanes_of(block)].astype(f32)
+
+    swap.wait_send()
+    fits = columns // (pair * tokens)
+
+    def outbox(which, turn, rows):
+        at, lane = turn // (positions // piece), turn % (positions // piece)
+        return cache.at[
+            which, at // fits, pl.ds(at % fits * pair * tokens, rows), pl.ds(lane * piece, piece)
+        ]
 
     def cross(turn):
         boths[turn].wait_recv()
+        box = outbox(0, turn, pair * tokens)
         for i, block in enumerate(twin_order):
-            outbox[turn, i] = added(turn, block).astype(bf16)
-        crosses[turn] = remote(
-            outbox.at[turn], inbox.at[turn], cross_send, cross_recv.at[turn], {"ep": twin}
-        )
+            box[i * tokens : (i + 1) * tokens, :] = added(turn, block).astype(bf16)
+        crosses[turn] = remote(box, inbox.at[turn], cross_send, cross_recv.at[turn], {"ep": twin})
         crosses[turn].start()
 
     def back(turn):
         crosses[turn].wait_recv()
+        box = outbox(1, turn, (pair - 1) * tokens)
         for i, block in enumerate(near_order):
-            total = added(turn, block) + inbox[turn, i].astype(f32)
+            rows = pl.ds(i * tokens, tokens)
+            total = added(turn, block) + inbox[turn, rows, :].astype(f32)
             if i == pair - 1:
-                totals[turn] = total
+                limits[turn * tokens : (turn + 1) * tokens, :piece] = total
                 continue
-            outbox2[turn, i] = total.astype(bf16)
-            remote(
-                outbox2.at[turn, i], inbox2.at[turn, i], back_send, back_recv.at[turn], {"ep": block}
-            ).start()
+            box[rows, :] = total.astype(bf16)
+            remote(box.at[rows, :], inbox2.at[turn, i], back_send, back_recv.at[turn], {"ep": block}).start()
 
     def end(turn):
-        total = totals[turn]
+        total = limits[turn * tokens : (turn + 1) * tokens, :piece]
         drain(inbox2.at[turn], back_recv.at[turn])
         for i in range(pair - 1):
             total = total + inbox2[turn, i].astype(f32)
-        out_ref[:, turn * piece : (turn + 1) * piece] = total.astype(bf16)
+        span = pl.ds(turn * piece, piece)
+        out_v[:, span] = total.astype(bf16)
+        copy_here(out_v.at[:, span], out_hbm.at[:, span], store_sem.at[1])
 
     for turn in range(turns + 3):
         if turn < turns:
@@ -666,19 +712,31 @@
             cross(turn - 1)
         if turn >= 3:
             back(turn - 3)
+    drain(heads_all.at[: count - 1], heads_send)
+    out_v = heads_own
     for turn in range(turns):
         end(turn)
 
     drain(values.at[:, : count - 1], value_send)
-    drain(heads_all.at[: count - 1], heads_send)
     pieces.finish()
-    swap.wait_send()
     drain(residual.at[: count - 1], res_sem.at[0])
     drain(ids_all.at[: count - 1], id_sem.at[0])
     drain(theirs, pair_send)
     drain(sums2, both_send)
     drain(inbox, cross_send)
     drain(inbox2, back_send)
+    drain(heads_own, store_sem.at[0])
+    drain(heads_own, store_sem.at[1])
+
+
+def store_kernel(hidden_hbm, out_hbm, hidden_to, out_to, hidden_v, out_v, in_sem, out_sem):
+    loads = [copy_here(hidden_hbm, hidden_v, in_sem.at[0]), copy_here(out_hbm, out_v, in_sem.at[1])]
+    loads[0].wait()
+    stores = [copy_here(hidden_v, hidden_to, out_sem.at[0])]
+    loads[1].wait()
+    stores.append(copy_here(out_v, out_to, out_sem.at[1]))
+    for copy in stores:
+        copy.wait()
 
 
 def dma(*shape):
@@ -716,16 +774,19 @@
     blocks = gate_weight.shape[0] // local
     hidden_here = gate_weight.shape[2]
     piece = model // 2 // TURNS
-    whole = pl.BlockSpec(memory_space=pltpu.VMEM)
     anywhere = pl.BlockSpec(memory_space=pl.ANY)
     vmem = pltpu.VMEM
     weight = (gate_weight.shape[0], hidden_here, model)
     hidden, expert_out = pl.pallas_call(
         functools.partial(layer_kernel, count),
         out_shape=(shape((tokens, model // 2), bf16), shape((tokens, model // 2), bf16)),
-        in_specs=[whole] * 4 + [anywhere] * 9,
-        out_specs=(whole, whole),
+        in_specs=[anywhere] * 13,
+        out_specs=(anywhere, anywhere),
         scratch_shapes=[
+            vmem((TOPK, tokens), jnp.int32),
+            vmem((1, tokens), jnp.int32),
+            vmem((1, tokens), jnp.int32),
+            vmem((1, model), f32),
             vmem((tokens * heads, columns), bf16),
             vmem((2, requests, columns, positions), bf16),
             vmem((heads, count) + value_proj.shape[1:], bf16),
@@ -740,38 +801,41 @@
             vmem((LATENT // 128, tokens * heads, 128), f32),
             vmem((tokens, heads * VDIM), bf16),
             vmem((count, tokens, heads * VDIM), bf16),
-            vmem((count, 2, tokens, width // 2), f32),
             vmem((count, tokens, width // 2), f32),
             vmem((count, count, 2, tokens, width // 2), bf16),
             vmem((count, 8, 128), jnp.int32),
             vmem((8, count * tokens), jnp.int32),
             vmem((count, local * CAP, tokens), bf16),
-            vmem((count * tokens, 128), f32),
             vmem((EXPERTS, count * tokens), f32),
+            vmem((local, slots), f32),
             vmem((local, 2 * blocks * hidden_here, slots), f32),
             vmem((count, tokens, local * CAP), bf16),
             vmem((local, slots, blocks * hidden_here), bf16),
-            vmem((TURNS, 2, count, tokens, piece), bf16),
-            vmem((TURNS, count, tokens, piece), bf16),
-            vmem((TURNS, far, tokens, piece), bf16),
-            vmem((TURNS, far, tokens, piece), bf16),
+            vmem((TURNS, tokens, count * piece), bf16),
+            vmem((TURNS, far * tokens, piece), bf16),
             vmem((TURNS, far - 1, tokens, piece), bf16),
-            vmem((TURNS, far - 1, tokens, piece), bf16),
-            vmem((TURNS, tokens, piece), f32),
-            dma(6), dma(local), dma(), dma(2), dma(2), dma(2),
+            dma(10), dma(), dma(), dma(2), dma(2), dma(2),
             dma(), dma(2, far, PARTS), dma(), dma(2, far, PARTS), dma(), dma(count),
             dma(), dma(count, 2, far), dma(), dma(count),
-            dma(), dma(TURNS), dma(), dma(TURNS), dma(), dma(TURNS),
+            dma(), dma(TURNS), dma(), dma(TURNS), dma(), dma(TURNS), dma(2),
         ],
         compiler_params=pltpu.CompilerParams(
-            collective_id=0, has_side_effects=True, vmem_limit_bytes=59 * 2**20
+            collective_id=0, has_side_effects=True, vmem_limit_bytes=56 * 2**20
         ),
     )(
-        expert_ids.T, token_visible[None], token_request[None], norm_gain.reshape(count, model // count), queries.reshape(tokens * heads, columns),
+        expert_ids.T, token_visible[None], token_request[None], norm_gain[None], queries.reshape(tokens * heads, columns),
         jnp.swapaxes(latent_cache, 1, 2), value_proj, out_proj, residual, router.T,
         jnp.swapaxes(gate_weight, 1, 2), jnp.swapaxes(up_weight, 1, 2), down_weight,
     )
-    return (hidden, expert_out)
+    half_block = vmem((tokens, model // 2), bf16)
+    return pl.pallas_call(
+        store_kernel,
+        out_shape=(shape((tokens, model // 2), bf16), shape((tokens, model // 2), bf16)),
+        in_specs=[anywhere] * 2,
+        out_specs=(anywhere, anywhere),
+        scratch_shapes=[half_block, half_block, dma(2), dma(2)],
+        compiler_params=pltpu.CompilerParams(vmem_limit_bytes=56 * 2**20),
+    )(hidden, expert_out)
 
 
 LEAN_BYTES = 8 * 2**20

time: 82.1 us -> 77.1 us (0.939)
  local copies, waits for them, and re-layouts: 4.43 us -> 0 us
    unnamed x2 -> x0, local copies, waits for them, and re-layouts: 3.14 us -> none
    pallas_call x1, Pallas kernels: 76.7 us -> 74.5 us  [lean_body(): pl.pallas_call(functools.partial(layer_kernel, count), out_shape=(shape((...]
    pallas_call x0 -> x1, Pallas kernels: none -> 1.66 us  [lean_body(): pl.pallas_call(store_kernel, out_shape=(shape((tokens, model // 2), bf16)...]
    reshape x1 -> x0, local copies, waits for them, and re-layouts: 1.3 us -> none  [lean_body(): norm_gain.reshape(count, model // count)]
where the time goes in v4:
time: 77.1 us; the launch traced here: 76.9 us
  Pallas kernels  76.1 us (99%)
  between operations  0.8 us (1%)
    pallas_call x1, Pallas kernels, lean_body(): pl.pallas_call(functools.partial(layer_kernel, count), out_shape=(shape((...  74.5 us
    pallas_call x1, Pallas kernels, lean_body(): pl.pallas_call(store_kernel, out_shape=(shape((tokens, model // 2), bf16)...  1.66 us

profile of v4, /device:TPU:0, one launch (start us, length us, event | category | flops | bytes accessed | tf_op | source)
XLA Modules:
  0.0 76.9 jit_solution(17595871806570049710)
XLA Ops:
  0.6 74.5 %shard_map.140 = (bf16[64,1024]{1,0:T(8,128)(2,1)}, bf16[64,1024]{1,0:T(8,128)(2,1)}) custom-call(s32[6,64]{1,0:T(8,128)} %bitcast.15, s32[1,64]{1,0:T(1,128)} %bitcast.16, s32[1,64]{1,0:T(1,128)} %bitcast.17, f32[1,2048]{1,0:T(1,128)} %bitcast.14, bf16[512,576]{1,0:T(8,128)(2,1)} %bitcast.12, bf16[3,576,256]{2,1,0:T(8,128)(2,1)} %bitcast.11, ...), custom_call_target="tpu_custom_call" | custom-call | tf_op jit(solution)/shard_map/pallas_call | solution.py:780
  75.1 1.7 %shard_map.141 = (bf16[64,1024]{1,0:T(8,128)(2,1)}, bf16[64,1024]{1,0:T(8,128)(2,1)}) custom-call(bf16[64,1024]{1,0:T(8,128)(2,1)} %get-tuple-element.4.hidden_hbm, bf16[64,1024]{1,0:T(8,128)(2,1)} %get-tuple-element.5.out_hbm), custom_call_target="tpu_custom_call" | custom-call | tf_op jit(solution)/shard_map/pallas_call | solution.py:831

commit v5 on v4

--- a/solution.py
+++ b/solution.py
@@ -426,19 +426,17 @@
         for piece in range(latent // 128):
             context[piece, rows, :] = summed[:, piece * 128 : (piece + 1) * 128]
 
-    value_ring.relay(1)
     swap.wait_recv()
     chunks = list(range(0, tokens * heads, ROWS))
-    done = 0
-    for step in range(2, far + 1):
-        until = -(-len(chunks) * (step - 1) // (far - 1)) if step < far else len(chunks)
-        for start in chunks[done:until]:
-            attend(start)
-        done = until
+    for step in range(1, far + 1):
+        if chunks:
+            attend(chunks.pop(0))
         value_ring.relay(step)
-        if step == 2:
+        if step == 3:
             for copy in spreads:
                 copy.start()
+    for start in chunks:
+        attend(start)
     for h in range(heads):
         rows = jnp.concatenate(
             [context[piece, pl.ds(h, tokens, stride=heads), :] for piece in range(latent // 128)], axis=1

time: 77.1 us -> 76.9 us (level)
  no operation moved by 1% of the time
where the time goes in v5:
time: 76.9 us; the launch traced here: 76.7 us
  Pallas kernels  75.9 us (99%)
  between operations  0.8 us (1%)
    pallas_call x1, Pallas kernels, lean_body(): pl.pallas_call(functools.partial(layer_kernel, count), out_shape=(shape((...  74.3 us
    pallas_call x1, Pallas kernels, lean_body(): pl.pallas_call(store_kernel, out_shape=(shape((tokens, model // 2), bf16)...  1.66 us

profile of v5, /device:TPU:0, one launch (start us, length us, event | category | flops | bytes accessed | tf_op | source)
XLA Modules:
  0.0 76.7 jit_solution(4979963344234577299)
XLA Ops:
  0.6 74.3 %shard_map.140 = (bf16[64,1024]{1,0:T(8,128)(2,1)}, bf16[64,1024]{1,0:T(8,128)(2,1)}) custom-call(s32[6,64]{1,0:T(8,128)} %bitcast.15, s32[1,64]{1,0:T(1,128)} %bitcast.16, s32[1,64]{1,0:T(1,128)} %bitcast.17, f32[1,2048]{1,0:T(1,128)} %bitcast.14, bf16[512,576]{1,0:T(8,128)(2,1)} %bitcast.12, bf16[3,576,256]{2,1,0:T(8,128)(2,1)} %bitcast.11, ...), custom_call_target="tpu_custom_call" | custom-call | tf_op jit(solution)/shard_map/pallas_call | solution.py:778
  74.9 1.7 %shard_map.141 = (bf16[64,1024]{1,0:T(8,128)(2,1)}, bf16[64,1024]{1,0:T(8,128)(2,1)}) custom-call(bf16[64,1024]{1,0:T(8,128)(2,1)} %get-tuple-element.4.hidden_hbm, bf16[64,1024]{1,0:T(8,128)(2,1)} %get-tuple-element.5.out_hbm), custom_call_target="tpu_custom_call" | custom-call | tf_op jit(solution)/shard_map/pallas_call | solution.py:829
